TPU v7x, 256 devices: a whole 4x4x8 slice. The times are simulated.
256 devices in a mesh: pipe: 2 (over x_hi), tensor: 8 (over y, core), seq: 16 (over z, x_lo).
Axes of the slice: x: 4 (x_hi: 2, x_lo: 2; x = x_hi * 2 + x_lo), y: 4, z: 8, core: 2. Of those that a mesh axis runs over, the one named last changes fastest.
Arguments:
- tokens: bfloat16 [2, 2048, 2560], P(None, 'seq', 'tensor'), may hold values from -6 to 6
- prenorm_gain: float32 [2, 2560], P('pipe'), may hold values from 0.5 to 1.5
- gate_weight: bfloat16 [2, 2560, 5120], P('pipe', None, 'tensor'), may hold values from -0.125 to 0.125
- inner_weight: bfloat16 [2, 2560, 5120], P('pipe', None, 'tensor'), may hold values from -0.125 to 0.125
- state_weight: bfloat16 [2, 2560, 256], P('pipe'), may hold values from -0.125 to 0.125
- step_weight: bfloat16 [2, 2560, 80], P('pipe', None, 'tensor'), may hold values from -0.125 to 0.125
- inner_taps: float32 [2, 5, 5120], P('pipe', None, 'tensor'), may hold values from -3 to 3
- state_taps: float32 [2, 5, 256], P('pipe'), may hold values from -3 to 3
- step_bias: float32 [2, 80], P('pipe', 'tensor'), may hold values from -5 to -2
- decay_rate: float32 [2, 80], P('pipe', 'tensor'), may hold values from 0.00048828125 to 1
- skip_scale: float32 [2, 80], P('pipe', 'tensor'), may hold values from 0.5 to 1.5
- inner_gain: float32 [2, 5120], P('pipe', 'tensor'), may hold values from 0.5 to 1.5
- out_weight: bfloat16 [2, 5120, 2560], P('pipe', 'tensor'), may hold values from -0.078125 to 0.078125
Outputs:
- layer_outputs: bfloat16 [2, 2, 2048, 2560], P('pipe', None, 'seq', 'tensor')
All inputs are finite; a program needn't handle non-finite values.
Results may differ from a plain program's by a relative error of at most 0.019.
Values may be sent and summed in bfloat16 or wider, within the bound.
A program may use at most 64 MiB of HBM per device.

v0:
```python
import jax
import jax.numpy as jnp
from jax import lax
from jax.sharding import Mesh
from jax.sharding import PartitionSpec as P

BLOCK = 128
INNER = 5120
SEQ = ("seq_0", "seq_1")


EPS = 1e-05


def shifted(value, axis, steps):
    count = lax.axis_size(axis)
    first, last = (max(0, -steps), min(count, count - steps))
    return lax.ppermute(value, axis, [(source, source + steps) for source in range(first, last)])


def neutral_like(array, identity):
    return jax.tree.map(
        lambda part, zero: jnp.zeros_like(part) + jnp.asarray(zero, part.dtype), array, identity
    )


def entering_2(array, axes, combine, identity):
    before = start = neutral_like(array, identity)
    running = array
    for axis in reversed(axes):
        size, here = (lax.axis_size(axis), lax.axis_index(axis))
        pieces = jax.tree.map(
            lambda part, kind: lax.all_gather(part.astype(kind), axis),
            running,
            (jnp.bfloat16, jnp.bfloat16),
        )
        inside, running = (start, start)
        for k in range(size):
            passed = k < here
            running = combine(
                running, jax.tree.map(lambda part, own: part[k].astype(own.dtype), pieces, array)
            )
            inside = jax.tree.map(lambda new, old: jnp.where(passed, new, old), running, inside)
        before = combine(inside, before)
    return before


def from_everyone(array, axis):
    size = lax.axis_size(axis)
    return lax.all_to_all(
        jnp.broadcast_to(array[None], (size, *array.shape)), axis, 0, 0, tiled=True
    )


def of_everyone(array, axis):
    everything = from_everyone(array, axis)
    return jnp.sum(everything, axis=0)


def joined_along(parts, dim):
    shape = list(parts.shape[1:])
    shape[dim] *= parts.shape[0]
    return jnp.moveaxis(parts, 0, dim).reshape(shape)


def collect(array, axis, dim):
    return joined_along(from_everyone(array, axis), dim)


def split_up(array, dim, size):
    shape = array.shape
    parts = array.reshape(*shape[:dim], size, shape[dim] // size, *shape[dim + 1 :])
    return jnp.moveaxis(parts, dim, 0)


def sent_and_summed(array, axis, dim):
    parts = split_up(array, dim, lax.axis_size(axis))
    arrived = lax.all_to_all(parts, axis, split_axis=0, concat_axis=0, tiled=True)
    return arrived.astype(jnp.float32).sum(axis=0)


def causal_taps(rim, values, taps):
    width = taps.shape[0] - 1
    length = values.shape[0]
    padded = jnp.concatenate([rim, values], axis=0).astype(jnp.float32)
    total = jnp.broadcast_to(taps[width][None, :], (length, values.shape[1]))
    for index in range(width):
        total = total + taps[index][None, :] * padded[index : index + length]
    return jax.nn.silu(total).astype(jnp.bfloat16)


def fold_states(carried, items):
    decay_acc, state_acc = carried
    decay, state = items
    return ((decay_acc * decay, state_acc * decay[:, None, None] + state), (decay_acc, state_acc))


def combine_states(earlier, later):
    return (earlier[0] * later[0], earlier[1] * later[0][:, None, None] + later[1])


def mixer(current, weights):
    (
        prenorm,
        gate_weight,
        inner_weight,
        state_weight,
        step_weight,
        inner_taps,
        state_taps,
        step_bias,
        decay_rate,
        skip_scale,
        inner_gain,
        out_weight,
    ) = weights
    rows = current.shape[0]
    widened = current.astype(jnp.float32)
    normed_in = (
        widened * lax.rsqrt(jnp.mean(widened * widened, axis=1, keepdims=True) + EPS) * prenorm
    ).astype(jnp.bfloat16)
    gate_raw = jnp.dot(normed_in, gate_weight, preferred_element_type=jnp.float32).astype(
        jnp.bfloat16
    )
    inner_raw = jnp.dot(normed_in, inner_weight, preferred_element_type=jnp.float32).astype(
        jnp.bfloat16
    )
    state_raw = jnp.dot(normed_in, state_weight, preferred_element_type=jnp.float32).astype(
        jnp.bfloat16
    )
    step_raw = jnp.dot(normed_in, step_weight, preferred_element_type=jnp.float32)
    inner_width = inner_raw.shape[1]
    reach = inner_taps.shape[0] - 2
    rim = shifted(
        jnp.concatenate([inner_raw[rows - reach :], state_raw[rows - reach :]], axis=1), SEQ, 1
    )
    inner_conv = causal_taps(rim[:, :inner_width], inner_raw, inner_taps)
    state_conv = causal_taps(rim[:, inner_width:], state_raw, state_taps)
    heads = step_bias.shape[0]
    head_size = inner_width // heads
    state_size = state_raw.shape[1] // 2
    blocks = rows // BLOCK
    step_size = jax.nn.softplus(step_raw + step_bias)
    step_blocks = step_size.reshape(blocks, BLOCK, heads)
    cumulative = jnp.cumsum(-step_blocks * decay_rate, axis=1)
    inner_blocks = inner_conv.reshape(blocks, BLOCK, heads, head_size)
    input_blocks = state_conv[:, :state_size].reshape(blocks, BLOCK, state_size)
    output_blocks = state_conv[:, state_size:].reshape(blocks, BLOCK, state_size)
    weighting = jnp.exp(cumulative[:, -1:, :] - cumulative) * step_blocks
    weighted = (inner_blocks.astype(jnp.float32) * weighting[..., None]).astype(jnp.bfloat16)
    states = jnp.einsum(
        "bshp,bsn->bhpn", weighted, input_blocks, preferred_element_type=jnp.float32
    )
    decays = jnp.exp(cumulative[:, -1, :])
    start = (
        jnp.ones((heads,), jnp.float32),
        jnp.zeros((heads, head_size, state_size), jnp.float32),
    )
    (device_decay, device_state), (prior_decay, prior_state) = lax.scan(
        fold_states, start, (decays, states)
    )
    entry_decay, entry_state = entering_2(
        (device_decay, device_state),
        SEQ,
        combine_states,
        (jnp.ones_like(device_decay), jnp.zeros_like(device_state)),
    )
    scores = jnp.einsum(
        "bqn,bsn->bqs", output_blocks, input_blocks, preferred_element_type=jnp.float32
    )
    by_head = jnp.transpose(cumulative, (0, 2, 1))
    later = lax.broadcasted_iota(jnp.int32, (BLOCK, BLOCK), 0) >= lax.broadcasted_iota(
        jnp.int32, (BLOCK, BLOCK), 1
    )
    decay = jnp.exp(jnp.where(later, by_head[:, :, :, None] - by_head[:, :, None, :], -jnp.inf))
    mixing = (
        scores[:, None] * decay * jnp.transpose(step_blocks, (0, 2, 1))[:, :, None, :]
    ).astype(jnp.bfloat16)
    inside = jnp.einsum("bhqs,bshp->bqhp", mixing, inner_blocks, preferred_element_type=jnp.float32)
    entering = prior_state + prior_decay[:, :, None, None] * entry_state[None]
    across = jnp.exp(cumulative)[..., None] * jnp.einsum(
        "bqn,bhpn->bqhp", output_blocks.astype(jnp.float32), entering
    )
    mixed = inside + across + skip_scale[None, None, :, None] * inner_blocks.astype(jnp.float32)
    mixed = mixed.reshape(rows, inner_width)
    gated = mixed * jax.nn.silu(gate_raw.astype(jnp.float32))
    squares = of_everyone(jnp.sum(gated * gated, axis=1), "tensor")
    normed = (gated * lax.rsqrt(squares / INNER + EPS)[:, None] * inner_gain).astype(jnp.bfloat16)
    return jnp.dot(normed, out_weight, preferred_element_type=jnp.float32)


def shards(
    tokens,
    prenorm_gain,
    gate_weight,
    inner_weight,
    state_weight,
    step_weight,
    inner_taps,
    state_taps,
    step_bias,
    decay_rate,
    skip_scale,
    inner_gain,
    out_weight,
):
    weights = (
        prenorm_gain[0],
        gate_weight[0],
        inner_weight[0],
        state_weight[0],
        step_weight[0],
        inner_taps[0],
        state_taps[0],
        step_bias[0],
        decay_rate[0],
        skip_scale[0],
        inner_gain[0],
        out_weight[0],
    )
    sections = lax.axis_size("pipe")
    section = lax.axis_index("pipe")
    share = lax.axis_size("tensor")
    member = lax.axis_index("tensor")
    all_tokens = collect(tokens, "tensor", 2)
    micro_count, rows, width = all_tokens.shape
    narrow = width // share
    outputs = jnp.zeros((micro_count, rows, narrow), jnp.bfloat16)
    carried = None
    rounds = micro_count + sections - 1
    for turn in range(rounds):
        fresh = all_tokens[min(turn, micro_count - 1)]
        if turn == 0:
            current = fresh
        else:
            incoming = collect(carried, "tensor", 1)
            current = jnp.where(section == 0, fresh, incoming)
        term = mixer(current, weights)
        summed = sent_and_summed(term.astype(jnp.bfloat16), "tensor", 1)
        base = lax.dynamic_slice_in_dim(current, member * narrow, narrow, 1)
        own = (base.astype(jnp.float32) + summed).astype(jnp.bfloat16)
        micro = turn - section
        valid = jnp.logical_and(micro >= 0, micro < micro_count)
        position = jnp.clip(micro, 0, micro_count - 1)
        previous = lax.dynamic_index_in_dim(outputs, position, 0, keepdims=False)
        outputs = lax.dynamic_update_index_in_dim(
            outputs, jnp.where(valid, own, previous), position, 0
        )
        if turn + 1 < rounds:
            carried = shifted(own, "pipe", 1)
    return outputs[None]


def solution(mesh):
    torus = Mesh(
        mesh.devices.reshape(mesh.shape["pipe"], mesh.shape["tensor"], 8, 2),
        ("pipe", "tensor", "seq_0", "seq_1"),
    )
    return jax.shard_map(
        shards,
        mesh=torus,
        in_specs=(
            P(None, SEQ, "tensor"),
            P("pipe", None),
            P("pipe", None, "tensor"),
            P("pipe", None, "tensor"),
            P("pipe", None, None),
            P("pipe", None, "tensor"),
            P("pipe", None, "tensor"),
            P("pipe", None, None),
            P("pipe", "tensor"),
            P("pipe", "tensor"),
            P("pipe", "tensor"),
            P("pipe", "tensor"),
            P("pipe", "tensor", None),
        ),
        out_specs=P("pipe", None, SEQ, "tensor"),
        check_vma=False,
    )
```

profile of v0, /device:TPU:6, one launch (start us, length us, event | category | flops | bytes accessed | tf_op | source)
XLA Modules:
  0.0 445.8 jit_solution(13413323776747706453)
XLA Ops:
  8.9 4.6 %all-to-all-start = ((bf16[8,2,128,320]{2,3,1,0:T(8,128)(2,1)}), bf16[8,2,128,320]{2,3,1,0:T(8,128)(2,1)}, u32[]{:S(2)}, u32[]{:S(2)}) async-start(bf16[8,2,128,320]{2,3,1,0:T(8,128)(2,1)} %broadcast_in_dim.70), calls=%async_computation | async-start | bytes 2621440 | tf_op jit(solution)/shard_map/all_to_all | solution.py:50
  14.9 17.4 %all-to-all-done = bf16[8,2,128,320]{2,3,1,0:T(8,128)(2,1)} async-done(((bf16[8,2,128,320]{2,3,1,0:T(8,128)(2,1)}), bf16[8,2,128,320]{2,3,1,0:T(8,128)(2,1)}, u32[]{:S(2)}, u32[]{:S(2)}) %all-to-all-start) | async-done | bytes 1310752 | tf_op jit(solution)/shard_map/all_to_all | solution.py:50
  43.4 4.1 collective-permute-start
  47.5 4.2 all-gather
  64.4 6.0 %all-gather.1 = bf16[20,64,128]{2,1,0:T(8,128)(2,1)S(1)} all-gather(bf16[10,64,128]{2,1,0:T(8,128)(2,1)S(1)} %fusion.39), channel_id=3, replica_groups=mesh['pipe'=2,'tensor'=8,'seq_0'=8,'seq_1'=2] {'seq_1'}, dimensions={0}, use_global_device_ids=true | all-gather | bytes 491520 | tf_op jit(solution)/shard_map/all_gather | solution.py:33
  74.8 17.0 %all-gather.6 = bf16[8,1,10]{2,1,0:T(2,128)(2,1)S(1)} all-gather(bf16[1,1,10]{2,1,0:T(2,128)(2,1)S(1)} %multiply_convert_fusion.23), channel_id=1, replica_groups=mesh['pipe'=2,'tensor'=8,'seq_0'=8,'seq_1'=2] {'seq_0'}, dimensions={0}, use_global_device_ids=true | all-gather | bytes 180 | tf_op jit(solution)/shard_map/all_gather | solution.py:33
  95.6 15.5 %all-gather.13.cloned.1.call-done = bf16[8,10,64,128]{3,2,1,0:T(8,128)(2,1)} async-done(((bf16[1,10,64,128]{3,2,1,0:T(8,128)(2,1)}), bf16[8,10,64,128]{3,2,1,0:T(8,128)(2,1)}) %all-gather.13.cloned.1.call-update) | async-done | bytes 1310736 | tf_op jit(solution)/shard_map/all_gather | solution.py:33
  116.5 3.6 multiply_reduce_fusion.2
  120.7 4.3 all-to-all-start.1
  125.0 5.2 %all-to-all-done.1 = f32[8,1,128]{2,1,0:T(1,128)S(1)} async-done(((f32[8,1,128]{2,1,0:T(1,128)}), f32[8,1,128]{2,1,0:T(1,128)S(1)}, u32[]{:S(2)}, u32[]{:S(2)}) %all-to-all-start.1) | async-done | bytes 4128 | tf_op jit(solution)/shard_map/all_to_all | solution.py:50
  135.0 4.2 all-to-all-start.2
  141.6 9.3 %all-to-all-done.2 = bf16[8,128,320]{1,2,0:T(8,128)(2,1)} async-done(((bf16[8,128,320]{1,2,0:T(8,128)(2,1)}), bf16[8,128,320]{1,2,0:T(8,128)(2,1)}, u32[]{:S(2)}, u32[]{:S(2)}) %all-to-all-start.2) | async-done | bytes 655392 | tf_op jit(solution)/shard_map/all_to_all | solution.py:78
  154.4 6.5 %collective-permute-done.1 = bf16[128,320]{0,1:T(8,128)(2,1)S(1)} collective-permute-done((bf16[128,320]{0,1:T(8,128)(2,1)S(1)}, bf16[128,320]{0,1:T(8,128)(2,1)S(1)}, u32[]{:S(2)}, u32[]{:S(2)}) %collective-permute-start.1) | collective-permute-done | bytes 81952 | tf_op jit(solution)/shard_map/ppermute | solution.py:18
  161.8 4.2 all-to-all-start.3
  166.1 11.7 %all-to-all-done.3 = bf16[8,128,320]{1,2,0:T(8,128)(2,1)} async-done(((bf16[8,128,320]{1,2,0:T(8,128)(2,1)}), bf16[8,128,320]{1,2,0:T(8,128)(2,1)}, u32[]{:S(2)}, u32[]{:S(2)}) %all-to-all-start.3) | async-done | bytes 655392 | tf_op jit(solution)/shard_map/all_to_all | solution.py:50
  196.7 4.2 all-gather.2
  214.5 6.0 %all-gather.3 = bf16[20,64,128]{2,1,0:T(8,128)(2,1)S(1)} all-gather(bf16[10,64,128]{2,1,0:T(8,128)(2,1)S(1)} %fusion.40), channel_id=5, replica_groups=mesh['pipe'=2,'tensor'=8,'seq_0'=8,'seq_1'=2] {'seq_1'}, dimensions={0}, use_global_device_ids=true | all-gather | bytes 491520 | tf_op jit(solution)/shard_map/all_gather | solution.py:33
  224.8 14.0 %all-gather.7 = bf16[8,1,10]{2,1,0:T(2,128)(2,1)S(1)} all-gather(bf16[1,1,10]{2,1,0:T(2,128)(2,1)S(1)} %multiply_convert_fusion.22), channel_id=1, replica_groups=mesh['pipe'=2,'tensor'=8,'seq_0'=8,'seq_1'=2] {'seq_0'}, dimensions={0}, use_global_device_ids=true | all-gather | bytes 180 | tf_op jit(solution)/shard_map/all_gather | solution.py:33
  245.1 13.4 %all-gather.15.cloned.1.call-done = bf16[8,10,64,128]{3,2,1,0:T(8,128)(2,1)} async-done(((bf16[1,10,64,128]{3,2,1,0:T(8,128)(2,1)}), bf16[8,10,64,128]{3,2,1,0:T(8,128)(2,1)}) %all-gather.15.cloned.1.call-update) | async-done | bytes 1310736 | tf_op jit(solution)/shard_map/all_gather | solution.py:33
  263.9 3.6 multiply_reduce_fusion.1
  267.5 9.4 %all_to_all.48 = f32[8,1,128]{2,1,0:T(1,128)S(1)} all-to-all(f32[8,1,128]{2,1,0:T(1,128)S(1)} %broadcast_in_dim.80), channel_id=1, replica_groups=mesh['pipe'=2,'tensor'=8,'seq_0'=8,'seq_1'=2] {'tensor'}, dimensions={0} | all-to-all | bytes 8192 | tf_op jit(solution)/shard_map/all_to_all | solution.py:50
  282.8 4.2 all-to-all-start.5
  287.7 11.0 %all-to-all-done.5 = bf16[8,128,320]{1,2,0:T(8,128)(2,1)} async-done(((bf16[8,128,320]{1,2,0:T(8,128)(2,1)}), bf16[8,128,320]{1,2,0:T(8,128)(2,1)}, u32[]{:S(2)}, u32[]{:S(2)}) %all-to-all-start.5) | async-done | bytes 655392 | tf_op jit(solution)/shard_map/all_to_all | solution.py:78
  302.3 6.5 %collective-permute-done.3 = bf16[128,320]{0,1:T(8,128)(2,1)S(1)} collective-permute-done((bf16[128,320]{0,1:T(8,128)(2,1)S(1)}, bf16[128,320]{0,1:T(8,128)(2,1)S(1)}, u32[]{:S(2)}, u32[]{:S(2)}) %collective-permute-start.3) | collective-permute-done | bytes 81952 | tf_op jit(solution)/shard_map/ppermute | solution.py:18
  308.9 14.2 %all_to_all.49 = bf16[8,128,320]{1,2,0:T(8,128)(2,1)S(1)} all-to-all(bf16[8,128,320]{1,2,0:T(8,128)(2,1)S(1)} %broadcast_in_dim.83), channel_id=1, replica_groups=mesh['pipe'=2,'tensor'=8,'seq_0'=8,'seq_1'=2] {'tensor'}, dimensions={0} | all-to-all | bytes 1310720 | tf_op jit(solution)/shard_map/all_to_all | solution.py:50
  337.1 4.2 all-gather.4
  354.1 6.0 %all-gather.5 = bf16[20,64,128]{2,1,0:T(8,128)(2,1)S(1)} all-gather(bf16[10,64,128]{2,1,0:T(8,128)(2,1)S(1)} %fusion.41), channel_id=7, replica_groups=mesh['pipe'=2,'tensor'=8,'seq_0'=8,'seq_1'=2] {'seq_1'}, dimensions={0}, use_global_device_ids=true | all-gather | bytes 491520 | tf_op jit(solution)/shard_map/all_gather | solution.py:33
  361.8 13.9 %all-gather.8 = bf16[8,1,10]{2,1,0:T(2,128)(2,1)S(1)} all-gather(bf16[1,1,10]{2,1,0:T(2,128)(2,1)S(1)} %multiply_convert_fusion.21), channel_id=1, replica_groups=mesh['pipe'=2,'tensor'=8,'seq_0'=8,'seq_1'=2] {'seq_0'}, dimensions={0}, use_global_device_ids=true | all-gather | bytes 180 | tf_op jit(solution)/shard_map/all_gather | solution.py:33
  381.2 16.4 %all-gather.17.cloned.1.call-done = bf16[8,10,64,128]{3,2,1,0:T(8,128)(2,1)} async-done(((bf16[1,10,64,128]{3,2,1,0:T(8,128)(2,1)}), bf16[8,10,64,128]{3,2,1,0:T(8,128)(2,1)}) %all-gather.17.cloned.1.call-update) | async-done | bytes 1310736 | tf_op jit(solution)/shard_map/all_gather | solution.py:33
  406.4 9.4 %all_to_all.50 = f32[8,1,128]{2,1,0:T(1,128)S(1)} all-to-all(f32[8,1,128]{2,1,0:T(1,128)S(1)} %broadcast_in_dim.84), channel_id=1, replica_groups=mesh['pipe'=2,'tensor'=8,'seq_0'=8,'seq_1'=2] {'tensor'}, dimensions={0} | all-to-all | bytes 8192 | tf_op jit(solution)/shard_map/all_to_all | solution.py:50
  420.6 4.2 all-to-all-start.8
  425.4 11.0 %all-to-all-done.8 = bf16[8,128,320]{1,2,0:T(8,128)(2,1)} async-done(((bf16[8,128,320]{1,2,0:T(8,128)(2,1)}), bf16[8,128,320]{1,2,0:T(8,128)(2,1)}, u32[]{:S(2)}, u32[]{:S(2)}) %all-to-all-start.8) | async-done | bytes 655392 | tf_op jit(solution)/shard_map/all_to_all | solution.py:78
  (293 shorter events, 162.4 us)
Async XLA Ops:
  6.5 123.7 %copy-start = (bf16[1,640,2560]{2,1,0:T(8,128)(2,1)S(1)}, bf16[1,640,2560]{2,1,0:T(8,128)(2,1)}, u32[]{:S(2)}) copy-start(bf16[1,640,2560]{2,1,0:T(8,128)(2,1)} %param.25) | copy-start | bytes 9830404
  8.9 5.4 %copy-start.41 = (f32[1,5,256]{2,0,1:T(1,128)S(1)}, f32[1,5,256]{2,0,1:T(1,128)}, u32[]{:S(2)}) copy-start(f32[1,5,256]{2,0,1:T(1,128)} %param.20) | copy-start | bytes 15364
  8.9 23.4 %all-to-all-start = ((bf16[8,2,128,320]{2,3,1,0:T(8,128)(2,1)}), bf16[8,2,128,320]{2,3,1,0:T(8,128)(2,1)}, u32[]{:S(2)}, u32[]{:S(2)}) async-start(bf16[8,2,128,320]{2,3,1,0:T(8,128)(2,1)} %broadcast_in_dim.70), calls=%async_computation | async-start | bytes 2621440 | tf_op jit(solution)/shard_map/all_to_all | solution.py:50
  13.5 22.7 %copy-start.16 = (bf16[1,2560,10]{1,2,0:T(8,128)(2,1)S(1)}, bf16[1,2560,10]{1,2,0:T(8,128)(2,1)}, u32[]{:S(2)}) copy-start(bf16[1,2560,10]{1,2,0:T(8,128)(2,1)} %param.18) | copy-start | bytes 153604
  13.5 22.6 %copy-start.42 = (f32[1,10]{1,0:T(1,128)S(1)}, f32[1,10]{1,0:T(1,128)}, u32[]{:S(2)}) copy-start(f32[1,10]{1,0:T(1,128)} %param.21) | copy-start | bytes 124
  13.5 97.6 %all-gather.13.cloned.1.call-start = ((), (), s32[]{:S(2)}) async-start(), calls=%async_computation.9 | async-start | bytes 1474560 | tf_op jit(solution)/shard_map/all_gather | solution.py:33
  41.6 5.8 %copy-start.63 = (bf16[1,1,10]{2,1,0:T(2,128)(2,1)S(1)}, bf16[1,1,10]{2,1,0:T(2,128)(2,1)}, u32[]{:S(2)}) copy-start(bf16[1,1,10]{2,1,0:T(2,128)(2,1)} %get-tuple-element.90) | copy-start | bytes 64
  41.6 10.1 %copy-start.33 = (f32[1,128,10]{1,2,0:T(8,128)S(1)}, f32[1,128,10]{1,2,0:T(8,128)}, u32[]{:S(2)}) copy-start(f32[1,128,10]{1,2,0:T(8,128)} %copy.135) | copy-start | bytes 15364
  41.7 10.0 %copy-start.57 = (f32[10]{0:T(128)S(1)}, f32[10]{0:T(128)}, u32[]{:S(2)}) copy-start(f32[10]{0:T(128)} %get-tuple-element.89) | copy-start | bytes 124
  43.4 12.7 %collective-permute-start = (bf16[3,896]{1,0:T(4,128)(2,1)}, bf16[3,896]{1,0:T(4,128)(2,1)}, u32[]{:S(2)}, u32[]{:S(2)}) collective-permute-start(bf16[3,896]{1,0:T(4,128)(2,1)} %pad_maximum_fusion), channel_id=1, source_target_pairs={{0,1},{1,2},{2,3},{3,4},{4,5},{5,6},{6,7},{7,8},{8,9},{9,10},{10,1... | collective-permute-start | bytes 16136 | tf_op jit(solution)/shard_map/ppermute | solution.py:18
  60.4 10.8 %copy-start.51 = (f32[10]{0:T(128)S(1)}, f32[10]{0:T(128)}, u32[]{:S(2)}) copy-start(f32[10]{0:T(128)} %get-tuple-element.128) | copy-start | bytes 124
  60.4 10.8 %copy-start.58 = (f32[10]{0:T(128)S(1)}, f32[10]{0:T(128)}, u32[]{:S(2)}) copy-start(f32[10]{0:T(128)} %fusion.405) | copy-start | bytes 124
  116.5 8.5 %copy-start.48 = (f32[1,640]{1,0:T(1,128)S(1)}, f32[1,640]{1,0:T(1,128)}, u32[]{:S(2)}) copy-start(f32[1,640]{1,0:T(1,128)} %param.24) | copy-start | bytes 7684
  120.7 9.5 %all-to-all-start.1 = ((f32[8,1,128]{2,1,0:T(1,128)}), f32[8,1,128]{2,1,0:T(1,128)S(1)}, u32[]{:S(2)}, u32[]{:S(2)}) async-start(f32[8,1,128]{2,1,0:T(1,128)} %broadcast_in_dim.77), calls=%async_computation.1 | async-start | bytes 8192 | tf_op jit(solution)/shard_map/all_to_all | solution.py:50
  125.0 7.8 %copy-start.31 = (f32[640]{0:T(1024)}, f32[640]{0:T(1024)S(1)}, u32[]{:S(2)}) copy-start(f32[640]{0:T(1024)S(1)} %reduce.12) | copy-start | bytes 7684
  135.0 15.9 %all-to-all-start.2 = ((bf16[8,128,320]{1,2,0:T(8,128)(2,1)}), bf16[8,128,320]{1,2,0:T(8,128)(2,1)}, u32[]{:S(2)}, u32[]{:S(2)}) async-start(bf16[8,128,320]{1,2,0:T(8,128)(2,1)} %bitcast.493), calls=%async_computation.2 | async-start | bytes 1310720 | tf_op jit(solution)/shard_map/all_to_all | solution.py:78
  153.1 7.8 %collective-permute-start.1 = (bf16[128,320]{0,1:T(8,128)(2,1)S(1)}, bf16[128,320]{0,1:T(8,128)(2,1)S(1)}, u32[]{:S(2)}, u32[]{:S(2)}) collective-permute-start(bf16[128,320]{0,1:T(8,128)(2,1)S(1)} %get-tuple-element.71), channel_id=1, source_target_pairs={{0,128},{1,129},{2,130},{3,131},{4,132},{5,133},{6,134},{7,135},{8... | collective-permute-start | bytes 245768 | tf_op jit(solution)/shard_map/ppermute | solution.py:18
  161.8 15.9 %all-to-all-start.3 = ((bf16[8,128,320]{1,2,0:T(8,128)(2,1)}), bf16[8,128,320]{1,2,0:T(8,128)(2,1)}, u32[]{:S(2)}, u32[]{:S(2)}) async-start(bf16[8,128,320]{1,2,0:T(8,128)(2,1)} %broadcast_in_dim.79), calls=%async_computation.3 | async-start | bytes 1310720 | tf_op jit(solution)/shard_map/all_to_all | solution.py:50
  166.0 92.5 %all-gather.15.cloned.1.call-start = ((), (), s32[]{:S(2)}) async-start(), calls=%async_computation.10 | async-start | bytes 1474560 | tf_op jit(solution)/shard_map/all_gather | solution.py:33
  193.2 12.8 %collective-permute-start.2 = (bf16[3,896]{1,0:T(4,128)(2,1)}, bf16[3,896]{1,0:T(4,128)(2,1)}, u32[]{:S(2)}, u32[]{:S(2)}) collective-permute-start(bf16[3,896]{1,0:T(4,128)(2,1)} %pad_maximum_fusion.1), channel_id=1, source_target_pairs={{0,1},{1,2},{2,3},{3,4},{4,5},{5,6},{6,7},{7,8},{8,9},{9,10},{10,1... | collective-permute-start | bytes 16136 | tf_op jit(solution)/shard_map/ppermute | solution.py:18
  263.9 14.2 %copy-start.32 = (f32[640]{0:T(1024)S(1)}, f32[640]{0:T(1024)}, u32[]{:S(2)}) copy-start(f32[640]{0:T(1024)} %copy-done.31) | copy-start | bytes 7684
  282.8 15.9 %all-to-all-start.5 = ((bf16[8,128,320]{1,2,0:T(8,128)(2,1)}), bf16[8,128,320]{1,2,0:T(8,128)(2,1)}, u32[]{:S(2)}, u32[]{:S(2)}) async-start(bf16[8,128,320]{1,2,0:T(8,128)(2,1)} %bitcast.495), calls=%async_computation.5 | async-start | bytes 1310720 | tf_op jit(solution)/shard_map/all_to_all | solution.py:78
  287.0 110.5 %all-gather.17.cloned.1.call-start = ((), (), s32[]{:S(2)}) async-start(), calls=%async_computation.11 | async-start | bytes 1474560 | tf_op jit(solution)/shard_map/all_gather | solution.py:33
  301.0 7.8 %collective-permute-start.3 = (bf16[128,320]{0,1:T(8,128)(2,1)S(1)}, bf16[128,320]{0,1:T(8,128)(2,1)S(1)}, u32[]{:S(2)}, u32[]{:S(2)}) collective-permute-start(bf16[128,320]{0,1:T(8,128)(2,1)S(1)} %get-tuple-element.60), channel_id=1, source_target_pairs={{0,128},{1,129},{2,130},{3,131},{4,132},{5,133},{6,134},{7,135},{8... | collective-permute-start | bytes 245768 | tf_op jit(solution)/shard_map/ppermute | solution.py:18
  330.0 20.3 %copy-start.27 = (f32[640]{0:T(1024)S(1)}, f32[640]{0:T(1024)}, u32[]{:S(2)}) copy-start(f32[640]{0:T(1024)} %get-tuple-element.48) | copy-start | bytes 7684
  330.0 20.3 %copy-start.29 = (f32[640]{0:T(1024)S(1)}, f32[640]{0:T(1024)}, u32[]{:S(2)}) copy-start(f32[640]{0:T(1024)} %get-tuple-element.56) | copy-start | bytes 7684
  333.6 12.0 %collective-permute-start.4 = (bf16[3,896]{1,0:T(4,128)(2,1)}, bf16[3,896]{1,0:T(4,128)(2,1)}, u32[]{:S(2)}, u32[]{:S(2)}) collective-permute-start(bf16[3,896]{1,0:T(4,128)(2,1)} %pad_maximum_fusion.2), channel_id=1, source_target_pairs={{0,1},{1,2},{2,3},{3,4},{4,5},{5,6},{6,7},{7,8},{8,9},{9,10},{10,1... | collective-permute-start | bytes 16136 | tf_op jit(solution)/shard_map/ppermute | solution.py:18
  350.3 10.5 %copy-start.49 = (f32[10]{0:T(128)S(1)}, f32[10]{0:T(128)}, u32[]{:S(2)}) copy-start(f32[10]{0:T(128)} %get-tuple-element.124) | copy-start | bytes 124
  350.3 10.5 %copy-start.59 = (f32[10]{0:T(128)S(1)}, f32[10]{0:T(128)}, u32[]{:S(2)}) copy-start(f32[10]{0:T(128)} %fusion.407) | copy-start | bytes 124
  351.3 10.5 %copy-start.54 = (bf16[2,1,10]{2,1,0:T(2,128)(2,1)S(1)}, bf16[2,1,10]{2,1,0:T(2,128)(2,1)}, u32[]{:S(2)}) copy-start(bf16[2,1,10]{2,1,0:T(2,128)(2,1)} %copy-done.53) | copy-start | bytes 124
  353.0 44.5 %copy-start.50 = (f32[10]{0:T(128)S(1)}, f32[10]{0:T(128)}, u32[]{:S(2)}) copy-start(f32[10]{0:T(128)} %get-tuple-element.124) | copy-start | bytes 124
  420.6 15.9 %all-to-all-start.8 = ((bf16[8,128,320]{1,2,0:T(8,128)(2,1)}), bf16[8,128,320]{1,2,0:T(8,128)(2,1)}, u32[]{:S(2)}, u32[]{:S(2)}) async-start(bf16[8,128,320]{1,2,0:T(8,128)(2,1)} %bitcast.494), calls=%async_computation.8 | async-start | bytes 1310720 | tf_op jit(solution)/shard_map/all_to_all | solution.py:78
  (46 other events, 112.3 us)
Sparse Core Ops, SparseCore 0:
  72.1 38.9 all-gather.12
  222.8 35.6 all-gather.14
  361.8 35.6 all-gather.16
where the time goes:
time: 450 us; the launch traced here: 446 us
  waiting for transfers between devices  124 us (28%)
  blocking collectives  108 us (24%)
  local copies, waits for them, and re-layouts  62.3 us (14%)
  other arithmetic  53.4 us (12%)
  matrix products  44.3 us (10%)
  starting transfers between devices  39.4 us (9%)
  between operations  13.9 us (3%)
    all_gather x9, blocking collectives, entering_2(): lax.all_gather(part.astype(kind), axis)  75.6 us
    all_gather x3, waiting for transfers between devices, entering_2(): lax.all_gather(part.astype(kind), axis)  45.3 us
    all_to_all x3, waiting for transfers between devices, from_everyone(): lax.all_to_all(jnp.broadcast_to(array[None], (size, *array.shape)), axis,...  34.3 us
    all_to_all x3, blocking collectives, from_everyone(): lax.all_to_all(jnp.broadcast_to(array[None], (size, *array.shape)), axis,...  32.9 us
    all_to_all x3, waiting for transfers between devices, sent_and_summed(): lax.all_to_all(parts, axis, split_axis=0, concat_axis=0, tiled=True)  31.3 us
    ppermute x5, starting transfers between devices, shifted(): lax.ppermute(value, axis, [(source, source + steps) for source in range(f...  13.6 us
    all_to_all x3, starting transfers between devices, from_everyone(): lax.all_to_all(jnp.broadcast_to(array[None], (size, *array.shape)), axis,...  13.1 us
    ppermute x5, waiting for transfers between devices, shifted(): lax.ppermute(value, axis, [(source, source + steps) for source in range(f...  13.1 us
  transfers between devices with their start and end apart: 14, of which 11 were waited for; matrix products, arithmetic and copies ran while one was open for 9% of the time, Pallas kernels for 0%

commit v1 on v0

v1 whole, which is shorter than its diff:
```python
import jax
import jax.numpy as jnp
from jax import lax
from jax.experimental import pallas as pl
from jax.experimental.pallas import tpu as pltpu
from jax.sharding import PartitionSpec as P

MESH = pl.DeviceIdType.MESH
F32, BF16 = jnp.float32, jnp.bfloat16
HIGHEST = lax.Precision.HIGHEST
EPS = 1e-05
SECTIONS, SHARE, SEQ = 2, 8, 16
CHIPS = SHARE // 2
MICRO, ROWS, WIDTH, INNER = 2, 128, 2560, 5120
NARROW = WIDTH // SHARE
LOCAL = INNER // SHARE
STATE = 128
HEADS = 10
TAPS = 4
SLAB = 384
OWNED = MICRO * STATE // SEQ
OWNERS = SEQ // MICRO
EDGE = 8
BOTH = MICRO * ROWS


def silu(value):
    return value / (1.0 + jnp.exp(-value))


def dot(a, b, **options):
    return jnp.dot(a, b, preferred_element_type=F32, **options)


def remote(src, dst, send, recv, device):
    return pltpu.make_async_remote_copy(
        src_ref=src, dst_ref=dst, send_sem=send, recv_sem=recv, device_id=device, device_id_type=MESH
    )


def kernel(
    tokens, pre_gain, gate_w, inner_w, state_w, step_w, inner_taps, state_taps, step_bias, decay_rate,
    skip_scale, inner_gain, out_w, out,
    x, xg, gains, wi, ws, wd, wg, wo, acc_i, acc_s, acc_d, acc_g, squares, padded, inner_conv, state_conv,
    steps, growth, mixed, decay, decays, sent, arrived, back, entering, normed, halves, partner_half, joined, totals,
    own, local_sem, gather_s, gather_r, rim_s, rim_r, decay_s, decay_r, state_s, state_r, enter_s, enter_r,
    half_s, half_r, total_s, total_r, pipe_s, pipe_r, out_sem,
):
    section, member, place = (lax.axis_index(name) for name in ("pipe", "tensor", "seq"))
    chip, core = member // 2, member % 2
    partner = member + 1 - 2 * core

    loads = [
        pltpu.make_async_copy(source.at[0], target, local_sem.at[index])
        for index, (source, target) in enumerate(
            ((inner_w, wi), (state_w, ws), (step_w, wd), (gate_w, wg), (out_w, wo))
        )
    ]
    fetch = pltpu.make_async_copy(tokens, x.at[member], local_sem.at[5])

    @pl.when(section == 0)
    def _():
        fetch.start()

    for load in loads:
        load.start()

    barrier = pltpu.get_barrier_semaphore()
    pl.semaphore_signal(barrier, inc=1, device_id={"tensor": partner}, device_id_type=MESH)
    pl.semaphore_signal(barrier, inc=1, device_id={"pipe": 1 - section}, device_id_type=MESH)
    for step in range(1, CHIPS):
        other = ((chip + step) % CHIPS) * 2 + core
        pl.semaphore_signal(barrier, inc=1, device_id={"tensor": other}, device_id_type=MESH)
    for step in range(1, SEQ):
        pl.semaphore_signal(barrier, inc=1, device_id={"seq": (place + step) % SEQ}, device_id_type=MESH)

    for k in range(SHARE):
        gains[k] = pre_gain[:, k * NARROW : (k + 1) * NARROW]
    steps[...] = jnp.zeros_like(steps)

    @pl.when(place == 0)
    def _():
        padded[:, 0:EDGE, :] = jnp.zeros((MICRO, EDGE, LOCAL + 2 * STATE), F32)
        entering[...] = jnp.zeros_like(entering)

    pl.semaphore_wait(barrier, 2 + CHIPS - 1 + SEQ - 1)

    handover = remote(own, x.at[member], pipe_s.at[0], pipe_r.at[0], {"pipe": 1})

    @pl.when(section == 0)
    def _():
        fetch.wait()

    @pl.when(section == 1)
    def _():
        handover.wait_recv()

    gathers = []
    for step in (2, 1, 3):
        other = ((chip + step) % CHIPS) * 2 + core
        gathers.append(
            remote(x.at[member], x.at[member], gather_s.at[step], gather_r.at[member], {"tensor": other})
        )
    gathers.append(
        remote(x.at[member], x.at[member], gather_s.at[0], gather_r.at[member], {"tensor": partner})
    )
    for copy in gathers:
        copy.start()
    for load in loads[:3]:
        load.wait()

    def project(index, carry):
        offset = lax.rem(index + 1, 3)
        turn = jnp.where(index < 2, 0, 1 + 2 * offset - 3 * (offset // 2))
        side = jnp.where(jnp.logical_or(index == 1, index > 4), 1 - core, core)
        which = lax.rem(chip + turn, CHIPS) * 2 + side
        block = x.at[which]

        @pl.when(index > 0)
        def _():
            remote(block, block, gather_s.at[0], gather_r.at[which], {"tensor": partner}).wait_recv()

        @pl.when(jnp.logical_and(index > 1, index < 5))
        def _():
            remote(
                block, block, gather_s.at[index + 2], gather_r.at[which], {"tensor": partner}
            ).start()

        wide = x[which].reshape(BOTH, NARROW).astype(F32)
        scaled = (wide * gains[which]).astype(BF16)
        xg[which] = scaled
        depth = pl.ds(pl.multiple_of(which * NARROW, 64), NARROW)
        square = jnp.sum(wide * wide, axis=1, keepdims=True)
        for target, weight in ((acc_i, wi), (acc_s, ws), (acc_d, wd)):
            term = dot(scaled, weight[depth, :])

            @pl.when(index == 0)
            def _():
                target[...] = term

            @pl.when(index > 0)
            def _():
                target[...] += term

        @pl.when(index == 0)
        def _():
            squares[...] = square

        @pl.when(index > 0)
        def _():
            squares[...] += square

        return carry

    lax.fori_loop(0, SHARE, project, 0)

    scale = lax.rsqrt(squares[...] / WIDTH + EPS)
    squares[...] = scale
    for micro in range(MICRO):
        part = slice(micro * ROWS, (micro + 1) * ROWS)
        padded[micro, EDGE : EDGE + ROWS, 0:LOCAL] = (acc_i[part, :] * scale[part]).astype(BF16).astype(F32)
        padded[micro, EDGE : EDGE + ROWS, LOCAL:] = (acc_s[part, :] * scale[part]).astype(BF16).astype(F32)
    rim = remote(
        padded.at[:, ROWS : ROWS + EDGE, :], padded.at[:, 0:EDGE, :], rim_s.at[0], rim_r.at[0],
        {"seq": lax.rem(place + 1, SEQ)},
    )

    @pl.when(place < SEQ - 1)
    def _():
        rim.start()

    shifted = acc_d[...] * scale + step_bias[...]
    steps[:, 0:HEADS] = jnp.maximum(shifted, 0.0) + jnp.log1p(jnp.exp(-jnp.abs(shifted)))

    loads[3].wait()

    def gate(index, carry):
        depth = pl.ds(pl.multiple_of(index * NARROW, 64), NARROW)
        term = dot(xg[index], wg[depth, :])

        @pl.when(index == 0)
        def _():
            acc_g[...] = term

        @pl.when(index > 0)
        def _():
            acc_g[...] += term

        return carry

    lax.fori_loop(0, SHARE, gate, 0)

    row = lax.broadcasted_iota(jnp.int32, (ROWS, ROWS), 0)
    lane = lax.broadcasted_iota(jnp.int32, (ROWS, ROWS), 1)
    first = lane < 64
    later = row >= lane

    @pl.when(place > 0)
    def _():
        rim.wait_recv()

    def send_states(owner):
        remote(
            decay.at[owner // OWNERS], decays.at[place], decay_s.at[owner], decay_r.at[place], {"seq": owner}
        ).start()
        remote(
            sent.at[owner], arrived.at[place], state_s.at[owner], state_r.at[place], {"seq": owner}
        ).start()

    for micro in range(MICRO):
        for column in range(0, LOCAL + 2 * STATE, 128):
            taps, at = (inner_taps, column) if column < LOCAL else (state_taps, column - LOCAL)
            total = jnp.broadcast_to(taps[0, TAPS : TAPS + 1, at : at + 128], (ROWS, 128))
            for index in range(TAPS):
                begin = EDGE - TAPS + 1 + index
                total = total + taps[0, index : index + 1, at : at + 128] * (
                    padded[micro, begin : begin + ROWS, column : column + 128]
                )
            result = silu(total).astype(BF16)
            if column < LOCAL:
                inner_conv[micro, :, at : at + 128] = result
            else:
                state_conv[micro, :, at : at + 128] = result

        part = slice(micro * ROWS, (micro + 1) * ROWS)
        rates = jnp.zeros((1, 128), F32)
        step_size = steps[part, :]
        rates = decays_row(decay_rate)
        cumulative = dot(later.astype(F32), -step_size * rates, precision=HIGHEST)
        across_step, across_sum = step_size.T, cumulative.T
        to_state = state_conv[micro, :, 0:STATE]
        from_state = state_conv[micro, :, STATE:]
        turned = to_state.astype(F32).T.astype(BF16)
        for pair in range(HEADS // 2):
            heads = (2 * pair, 2 * pair + 1)
            at = slice(pair * 128, pair * 128 + 128)
            sums = [jnp.broadcast_to(cumulative[:, h : h + 1], (ROWS, 128)) for h in heads]
            sizes = [jnp.broadcast_to(step_size[:, h : h + 1], (ROWS, 128)) for h in heads]
            each = jnp.where(first, sums[0], sums[1])
            values = inner_conv[micro, :, at].astype(F32)
            weighting = jnp.exp(each[ROWS - 1 :, :] - each) * jnp.where(first, sizes[0], sizes[1])
            state = dot(turned, (values * weighting).astype(BF16)).astype(BF16)
            sent[micro * OWNERS : (micro + 1) * OWNERS, :, at] = state.reshape(OWNERS, OWNED, 128)
            grown = jnp.exp(each)
            growth[micro, :, at] = grown
            decay[micro, :, at] = grown[ROWS - 1 :, :]

        for owner in range(micro * OWNERS, (micro + 1) * OWNERS):

            @pl.when(jnp.logical_and(place != owner, place < SEQ - 1))
            def _():
                send_states(owner)

        scores = lax.dot_general(
            from_state, to_state, (((1,), (1,)), ((), ())), preferred_element_type=F32
        )
        for pair in range(HEADS // 2):
            at = slice(pair * 128, pair * 128 + 128)
            values = inner_conv[micro, :, at]
            parts = []
            for h in (2 * pair, 2 * pair + 1):
                column = jnp.broadcast_to(cumulative[:, h : h + 1], (ROWS, 128))
                fade = jnp.exp(jnp.where(later, column - across_sum[h : h + 1, :], -jnp.inf))
                mixing = (scores * fade * across_step[h : h + 1, :]).astype(BF16)
                parts.append(dot(mixing, values))
            skip = jnp.where(first[0:1], skip_scale[0, 2 * pair], skip_scale[0, 2 * pair + 1])
            mixed[micro, :, at] = jnp.where(first, parts[0], parts[1]) + skip * values.astype(F32)

    arrived[place] = sent[place]
    decays[place] = decay[place // OWNERS]
    carried = jnp.zeros((OWNED, LOCAL), F32)
    for source in range(SEQ):
        if source > 0:
            back[source] = carried.astype(BF16)

            @pl.when(place != source)
            def _():
                remote(
                    back.at[source], entering.at[place], enter_s.at[source], enter_r.at[place],
                    {"seq": source},
                ).start()

        if source < SEQ - 1:

            @pl.when(place != source)
            def _():
                remote(
                    sent.at[source], arrived.at[source], state_s.at[source], state_r.at[source],
                    {"seq": source},
                ).wait_recv()
                remote(
                    decay.at[0], decays.at[source], decay_s.at[source], decay_r.at[source], {"seq": source}
                ).wait_recv()

            carried = decays[source] * carried + arrived[source].astype(F32)

    @pl.when(place > 0)
    def _():
        entering[place] = back[place]

    for micro in range(MICRO):
        for owner in range(micro * OWNERS, (micro + 1) * OWNERS):

            @pl.when(jnp.logical_and(place != owner, place > 0))
            def _():
                remote(
                    back.at[owner], entering.at[owner], enter_s.at[owner], enter_r.at[owner], {"seq": owner}
                ).wait_recv()

        part = slice(micro * ROWS, (micro + 1) * ROWS)
        from_state = state_conv[micro, :, STATE:]
        scale = squares[part, :]
        square = jnp.zeros((ROWS, 1), F32)
        for column in range(0, LOCAL, 128):
            at = slice(column, column + 128)
            entry = entering[micro * OWNERS : (micro + 1) * OWNERS, :, at].reshape(STATE, 128)
            value = mixed[micro, :, at] + growth[micro, :, at] * dot(from_state, entry)
            raw = (acc_g[part, at] * scale).astype(BF16).astype(F32)
            gated = value * silu(raw)
            square = square + jnp.sum(gated * gated, axis=1, keepdims=True)
            normed[part, at] = (gated * inner_gain[:, at]).astype(BF16)
        squares[part, :] = square

    loads[4].wait()
    wide_lane = lax.broadcasted_iota(jnp.int32, (BOTH, SLAB), 1)

    def with_squares(values, total):
        high = total.astype(BF16).astype(F32)
        spare = jnp.where(wide_lane < NARROW + 32, high, total - high)
        return jnp.where(wide_lane < NARROW, values, spare).astype(BF16)

    def to_partner(which):
        return remote(
            halves.at[1 - core, which], partner_half.at[which], half_s.at[which], half_r.at[which],
            {"tensor": partner},
        )

    def to_chip(which):
        return remote(
            joined.at[which], totals.at[chip], total_s.at[which], total_r.at[chip],
            {"tensor": which * 2 + core},
        )

    def spread(index, carry):
        which = lax.rem(chip + 1 + index, CHIPS)
        at = pl.ds(pl.multiple_of(which * 2 * NARROW, 128), 2 * NARROW)
        product = dot(normed[...], wo[:, at])
        turned = pltpu.roll(product, NARROW, 1)
        halves[0, which] = with_squares(product[:, 0:SLAB], squares[...])
        halves[1, which] = with_squares(turned[:, 0:SLAB], squares[...])
        to_partner(which).start()
        return carry

    lax.fori_loop(0, CHIPS, spread, 0)

    def join(index, carry):
        which = lax.rem(chip + 1 + index, CHIPS)
        to_partner(which).wait_recv()
        both = halves[core, which].astype(F32) + partner_half[which].astype(F32)
        total = both[:, NARROW : NARROW + 1] + both[:, NARROW + 32 : NARROW + 33]
        joined[which] = with_squares(both, total)

        @pl.when(index < CHIPS - 1)
        def _():
            to_chip(which).start()

        return carry

    lax.fori_loop(0, CHIPS, join, 0)

    total = joined[chip].astype(F32)
    for step in range(1, CHIPS):
        which = lax.rem(chip + step, CHIPS)
        remote(
            joined.at[which], totals.at[which], total_s.at[which], total_r.at[which],
            {"tensor": which * 2 + core},
        ).wait_recv()
        total = total + totals[which].astype(F32)
    square = total[:, NARROW : NARROW + 1] + total[:, NARROW + 32 : NARROW + 33]
    scale = lax.rsqrt(square / INNER + EPS)
    base = x[member].reshape(BOTH, NARROW).astype(F32)
    own[...] = (base + total[:, 0:NARROW] * scale).astype(BF16).reshape(MICRO, ROWS, NARROW)

    @pl.when(section == 0)
    def _():
        handover.start()

    write = pltpu.make_async_copy(own, out.at[0], out_sem.at[0])
    write.start()

    for copy in gathers:
        copy.wait_send()
    for index in range(2, 5):
        remote(
            x.at[member], x.at[member], gather_s.at[index + 2], gather_r.at[member], {"tensor": partner}
        ).wait_send()

    @pl.when(place < SEQ - 1)
    def _():
        rim.wait_send()

    for owner in range(SEQ):

        @pl.when(jnp.logical_and(place != owner, place < SEQ - 1))
        def _():
            remote(
                decay.at[0], decays.at[owner], decay_s.at[owner], decay_r.at[owner], {"seq": owner}
            ).wait_send()
            remote(
                sent.at[owner], arrived.at[owner], state_s.at[owner], state_r.at[owner], {"seq": owner}
            ).wait_send()

        if owner > 0:

            @pl.when(place != owner)
            def _():
                remote(
                    back.at[owner], entering.at[owner], enter_s.at[owner], enter_r.at[owner], {"seq": owner}
                ).wait_send()

    for step in range(CHIPS):
        which = lax.rem(chip + step, CHIPS)
        to_partner(which).wait_send()
        if step > 0:
            to_chip(which).wait_send()

    @pl.when(section == 0)
    def _():
        handover.wait_send()

    write.wait()


def decays_row(rate):
    return jnp.concatenate([rate[...], jnp.zeros((1, 128 - HEADS), F32)], axis=1)


def shards(*arrays):
    vmem, hbm, smem = (pl.BlockSpec(memory_space=space) for space in (pltpu.VMEM, pl.ANY, pltpu.SMEM))
    dma = lambda count: pltpu.SemaphoreType.DMA((count,))
    return pl.pallas_call(
        kernel,
        out_shape=jax.ShapeDtypeStruct((1, MICRO, ROWS, NARROW), BF16),
        in_specs=[hbm, vmem, hbm, hbm, hbm, hbm, vmem, vmem, vmem, vmem, smem, vmem, hbm],
        out_specs=hbm,
        scratch_shapes=[
            pltpu.VMEM((SHARE, MICRO, ROWS, NARROW), BF16),
            pltpu.VMEM((SHARE, BOTH, NARROW), BF16),
            pltpu.VMEM((SHARE, 1, NARROW), F32),
            pltpu.VMEM((WIDTH, LOCAL), BF16),
            pltpu.VMEM((WIDTH, 2 * STATE), BF16),
            pltpu.VMEM((WIDTH, HEADS), BF16),
            pltpu.VMEM((WIDTH, LOCAL), BF16),
            pltpu.VMEM((LOCAL, WIDTH), BF16),
            pltpu.VMEM((BOTH, LOCAL), F32),
            pltpu.VMEM((BOTH, 2 * STATE), F32),
            pltpu.VMEM((BOTH, HEADS), F32),
            pltpu.VMEM((BOTH, LOCAL), F32),
            pltpu.VMEM((BOTH, 1), F32),
            pltpu.VMEM((MICRO, EDGE + ROWS, LOCAL + 2 * STATE), F32),
            pltpu.VMEM((MICRO, ROWS, LOCAL), BF16),
            pltpu.VMEM((MICRO, ROWS, 2 * STATE), BF16),
            pltpu.VMEM((BOTH, 128), F32),
            pltpu.VMEM((MICRO, ROWS, LOCAL), F32),
            pltpu.VMEM((MICRO, ROWS, LOCAL), F32),
            pltpu.VMEM((MICRO, 1, LOCAL), F32),
            pltpu.VMEM((SEQ, 1, LOCAL), F32),
            pltpu.VMEM((SEQ, OWNED, LOCAL), BF16),
            pltpu.VMEM((SEQ, OWNED, LOCAL), BF16),
            pltpu.VMEM((SEQ, OWNED, LOCAL), BF16),
            pltpu.VMEM((SEQ, OWNED, LOCAL), BF16),
            pltpu.VMEM((BOTH, LOCAL), BF16),
            pltpu.VMEM((2, CHIPS, BOTH, SLAB), BF16),
            pltpu.VMEM((CHIPS, BOTH, SLAB), BF16),
            pltpu.VMEM((CHIPS, BOTH, SLAB), BF16),
            pltpu.VMEM((CHIPS, BOTH, SLAB), BF16),
            pltpu.VMEM((MICRO, ROWS, NARROW), BF16),
            dma(6), dma(7), dma(SHARE), dma(1), dma(1), dma(SEQ), dma(SEQ), dma(SEQ), dma(SEQ), dma(SEQ), dma(SEQ),
            dma(CHIPS), dma(CHIPS), dma(CHIPS), dma(CHIPS), dma(1), dma(1), dma(1),
        ],
        compiler_params=pltpu.CompilerParams(
            collective_id=0, has_side_effects=True, vmem_limit_bytes=48 * 1024 * 1024
        ),
    )(*arrays)


def solution(mesh):
    return jax.shard_map(
        shards,
        mesh=mesh,
        in_specs=(
            P(None, "seq", "tensor"),
            P("pipe", None),
            P("pipe", None, "tensor"),
            P("pipe", None, "tensor"),
            P("pipe", None, None),
            P("pipe", None, "tensor"),
            P("pipe", None, "tensor"),
            P("pipe", None, None),
            P("pipe", "tensor"),
            P("pipe", "tensor"),
            P("pipe", "tensor"),
            P("pipe", "tensor"),
            P("pipe", "tensor", None),
        ),
        out_specs=P("pipe", None, "seq", "tensor"),
        check_vma=False,
    )
```

time: 450 us -> 138 us (0.31)
  the two profiles are of different devices: /device:TPU:6 before, /device:TPU:102 now
where the time goes in v1:
time: 138 us; the launch traced here: 137 us
  Pallas kernels  126 us (91%)
  local copies, waits for them, and re-layouts  11.1 us (8%)
    pallas_call x1, Pallas kernels, shards(): pl.pallas_call(kernel, out_shape=jax.ShapeDtypeStruct((1, MICRO, ROWS, NA...  126 us
    unnamed x18, local copies, waits for them, and re-layouts  10.3 us

profile of v1, /device:TPU:102, one launch (start us, length us, event | category | flops | bytes accessed | tf_op | source)
XLA Modules:
  0.0 137.2 jit_solution(6432295194324323837)
XLA Ops:
  0.0 0.7 copy.17.state_taps
  0.7 0.7 copy.16.inner_taps
  1.4 1.1 copy.14.tokens
  2.5 1.3 copy.15.step_w
  3.7 0.0 copy-start
  3.7 1.9 %copy-done = bf16[1,2560,640]{2,1,0:T(8,128)(2,1)S(1)} copy-done((bf16[1,2560,640]{2,1,0:T(8,128)(2,1)S(1)}, bf16[1,2560,640]{2,1,0:T(8,128)(2,1)}, u32[]{:S(2)}) %copy-start) | copy-done | bytes 3276824
  5.7 0.0 copy-start.1
  5.7 1.3 copy-done.1
  7.0 0.0 copy-start.2
  7.0 0.7 copy-done.2
  7.7 0.0 copy-start.3
  7.7 0.7 copy-done.3
  8.4 0.0 copy-start.4
  8.4 0.7 copy-done.4
  9.0 0.0 copy-start.5
  9.0 0.7 copy-done.5
  9.7 0.0 copy-start.6
  9.7 0.7 copy-done.6
  10.3 126.1 %shard_map.127 = bf16[1,2,128,320]{3,2,1,0:T(8,128)(2,1)S(1)} custom-call(bf16[2,128,320]{2,1,0:T(8,128)(2,1)S(1)} %copy.14.tokens, f32[1,2560]{1,0:T(1,128)S(1)} %copy-done.2, bf16[1,2560,640]{2,1,0:T(8,128)(2,1)S(1)} %copy-done, bf16[1,2560,640]{2,1,0:T(8,128)(2,1)} %inner_w.1, bf16[1,2560,256]{2,1,0:T(8,128)(2,1)S(1)} %copy-done.1, ...), custom_call_target="tpu_custom_call" | custom-call | tf_op jit(solution)/shard_map/pallas_call | solution.py:441
  136.4 0.8 copy.18
Async XLA Ops:
  3.7 1.9 %copy-start = (bf16[1,2560,640]{2,1,0:T(8,128)(2,1)S(1)}, bf16[1,2560,640]{2,1,0:T(8,128)(2,1)}, u32[]{:S(2)}) copy-start(bf16[1,2560,640]{2,1,0:T(8,128)(2,1)} %gate_w.1) | copy-start | bytes 9830404
  5.7 1.3 copy-start.1
  7.0 0.7 copy-start.2
  7.7 0.7 copy-start.3
  8.4 0.7 copy-start.4
  9.0 0.7 copy-start.5
  9.7 0.7 copy-start.6

commit v2 on v1

v2 whole, which is shorter than its diff:
```python
import jax
import jax.numpy as jnp
from jax import lax
from jax.experimental import pallas as pl
from jax.experimental.pallas import tpu as pltpu
from jax.sharding import PartitionSpec as P

MESH = pl.DeviceIdType.MESH
F32, BF16 = jnp.float32, jnp.bfloat16
HIGHEST = lax.Precision.HIGHEST
EPS = 1e-05
SHARE, SEQ = 8, 16
CHIPS = SHARE // 2
MICRO, ROWS, WIDTH, INNER = 2, 128, 2560, 5120
NARROW = WIDTH // SHARE
PAIR = 2 * NARROW
LOCAL = INNER // SHARE
STATE = 128
BOTH = LOCAL + 2 * STATE
HEADS = 10
TAPS = 4
SLAB = NARROW + 16
OWNED = MICRO * STATE // SEQ
OWNERS = SEQ // MICRO
EDGE = 8
SENDS = 7


def silu(value):
    return value / (1.0 + jnp.exp(-value))


def dot(a, b, **options):
    return jnp.dot(a, b, preferred_element_type=F32, **options)


def dot_turned(a, b):
    return lax.dot_general(a, b, (((1,), (1,)), ((), ())), preferred_element_type=F32)


def remote(src, dst, send, recv, device):
    return pltpu.make_async_remote_copy(
        src_ref=src, dst_ref=dst, send_sem=send, recv_sem=recv, device_id=device, device_id_type=MESH
    )


def kernel(
    tokens, pre_gain_h, gate_h, inner_h, state_h, step_h, inner_taps_h, state_taps_h, bias_h, rate_h, skip_h, gain_h,
    out_h, out,
    x, xg, w1, wd, wg, wo, pre_gain, inner_taps, state_taps, bias, rate, skip_scale, inner_gain,
    acc, acc_d, gate_act, squares, scales, padded, inner_conv, state_conv, steps, sums, growth, mixed, decay, decays, sent,
    arrived, back, entering, normed, halves, partner_half, joined, before, totals, own, relay,
    local_s, gather_s, gather_r, rim_s, rim_r, decay_s, decay_r, state_s, state_r, enter_s, enter_r, half_s, half_r,
    before_s, before_r, total_s, total_r, pipe_s, pipe_r, pass_s, pass_r, out_s,
):
    section, member, place = (lax.axis_index(name) for name in ("pipe", "tensor", "seq"))
    chip, core = member // 2, member % 2
    partner = member + 1 - 2 * core
    beside = place + 1 - 2 * lax.rem(place, 2)
    after, behind, across_ring = (lax.rem(chip + step, CHIPS) for step in (1, CHIPS - 1, 2))

    def device(which):
        return {"tensor": which * 2 + core}

    loads = [
        pltpu.make_async_copy(source, target, local_s.at[index])
        for index, (source, target) in enumerate(
            (
                (tokens.at[0], x.at[chip, 0, core]),
                (tokens.at[1], x.at[chip, 1, core]),
                (inner_h.at[0], w1.at[:, 0:LOCAL]),
                (state_h.at[0], w1.at[:, LOCAL:BOTH]),
                (step_h.at[0], wd),
                (pre_gain_h, pre_gain),
                (inner_taps_h, inner_taps),
                (state_taps_h, state_taps),
                (bias_h, bias),
                (rate_h, rate),
                (skip_h, skip_scale),
                (gain_h, inner_gain),
                (gate_h.at[0], wg),
                (out_h.at[0], wo),
            )
        )
    ]

    @pl.when(section == 0)
    def _():
        for load in loads[:MICRO]:
            load.start()

    for load in loads[MICRO:]:
        load.start()

    barrier = pltpu.get_barrier_semaphore()

    def greet(peer):
        pl.semaphore_signal(barrier, inc=1, device_id=peer, device_id_type=MESH)

    for step in range(1, SEQ):
        greet({"seq": lax.rem(place + step, SEQ)})
    greet({"pipe": 1 - section, "seq": beside})
    greet(device(after))
    greet(device(behind))
    greet({"tensor": partner})

    steps[...] = jnp.zeros_like(steps)

    @pl.when(place == 0)
    def _():
        padded[:, 0:EDGE, :] = jnp.zeros((MICRO, EDGE, BOTH), F32)
        entering[...] = jnp.zeros_like(entering)

    pl.semaphore_wait(barrier, SEQ - 1 + 4)

    def handover(micro):
        return remote(
            own.at[micro], relay.at[micro], pipe_s.at[micro], pipe_r.at[micro], {"pipe": 1, "seq": beside}
        )

    def passing(micro):
        return remote(
            relay.at[micro], x.at[chip, micro, core], pass_s.at[micro], pass_r.at[micro], {"seq": beside}
        )

    def slab(which, side, micro, target, send):
        block = x.at[which, micro, side]
        return remote(
            block, block, gather_s.at[micro * SENDS + send], gather_r.at[(which * 2 + side) * MICRO + micro], target
        )

    to_partner = {"tensor": partner}

    def gather(micro, send):
        onward, backward = (behind, after) if micro == 0 else (after, behind)
        which, side, target = (
            (chip, core, device(after)),
            (chip, core, device(behind)),
            (chip, core, to_partner),
            (onward, core, device(backward)),
            (onward, core, to_partner),
            (backward, core, to_partner),
            (across_ring, core, to_partner),
        )[send]
        return slab(which, side, micro, target, send)

    def send_own(micro):
        @pl.when(section == 0)
        def _():
            loads[micro].wait()

        @pl.when(section == 1)
        def _():
            handover(micro).wait_recv()
            passing(micro).start()
            passing(micro).wait_recv()

        for send in range(3):
            gather(micro, send).start()

    def forward_near(micro):
        gather(micro, 4).wait_recv()
        gather(micro, 3).start()
        gather(micro, 4).start()
        gather(micro, 5).wait_recv()
        gather(micro, 5).start()

    def forward_far(micro):
        copy = gather(micro, 6)
        copy.wait_recv()
        copy.start()

    def project(micro, which, first):
        slab(which, 1 - core, micro, to_partner, 0).wait_recv()
        wide = x[which, micro].reshape(PAIR, ROWS).astype(F32).T
        at = pl.ds(pl.multiple_of(which * PAIR, 128), PAIR)
        scaled = (wide * pre_gain[:, at]).astype(BF16)
        xg[micro, :, at] = scaled
        square = wide * wide
        square = sum(square[:, column : column + 128] for column in range(0, PAIR, 128))
        term = dot(scaled, w1[at, :])
        term_d = dot_turned(scaled, wd[:, at])
        if first:
            acc[micro], acc_d[micro], squares[micro] = term, term_d, square
        else:
            acc[micro] += term
            acc_d[micro] += term_d
            squares[micro] += square

    def rim(micro):
        return remote(
            padded.at[micro, ROWS : ROWS + EDGE, :], padded.at[micro, 0:EDGE, :], rim_s.at[micro], rim_r.at[micro],
            {"seq": lax.rem(place + 1, SEQ)},
        )

    def project_end(micro):
        scale = lax.rsqrt(jnp.sum(squares[micro], axis=1, keepdims=True) / WIDTH + EPS)
        scales[micro] = scale
        padded[micro, EDGE : EDGE + ROWS, :] = (acc[micro] * scale).astype(BF16).astype(F32)

        @pl.when(place < SEQ - 1)
        def _():
            rim(micro).start()

        shifted = acc_d[micro] * scale + bias[...]
        steps[micro, :, 0:HEADS] = jnp.maximum(shifted, 0.0) + jnp.log1p(jnp.exp(-jnp.abs(shifted)))

    row = lax.broadcasted_iota(jnp.int32, (ROWS, ROWS), 0)
    lane = lax.broadcasted_iota(jnp.int32, (ROWS, ROWS), 1)
    first_half = lane < 64
    later = row >= lane

    def states(micro):
        rates = jnp.concatenate([rate[...], jnp.zeros((1, 128 - HEADS), F32)], axis=1)
        step_size = steps[micro]
        cumulative = dot(later.astype(F32), -step_size * rates, precision=HIGHEST)
        sums[micro] = cumulative

        @pl.when(place > 0)
        def _():
            rim(micro).wait_recv()

        for column in range(0, BOTH, 128):
            taps, at = (inner_taps, column) if column < LOCAL else (state_taps, column - LOCAL)
            total = jnp.broadcast_to(taps[TAPS, :, at : at + 128], (ROWS, 128))
            for index in range(TAPS):
                begin = EDGE - TAPS + 1 + index
                total = total + taps[index, :, at : at + 128] * (
                    padded[micro, begin : begin + ROWS, column : column + 128]
                )
            result = silu(total).astype(BF16)
            if column < LOCAL:
                inner_conv[micro, :, at : at + 128] = result
            else:
                state_conv[micro, :, at : at + 128] = result

        turned = state_conv[micro, :, 0:STATE].astype(F32).T.astype(BF16)
        for pair in range(HEADS // 2):
            heads = (2 * pair, 2 * pair + 1)
            at = slice(pair * 128, pair * 128 + 128)
            spread = [jnp.broadcast_to(cumulative[:, h : h + 1], (ROWS, 128)) for h in heads]
            sizes = [jnp.broadcast_to(step_size[:, h : h + 1], (ROWS, 128)) for h in heads]
            each = jnp.where(first_half, spread[0], spread[1])
            values = inner_conv[micro, :, at].astype(F32)
            weighting = jnp.exp(each[ROWS - 1 :, :] - each) * jnp.where(first_half, sizes[0], sizes[1])
            state = dot(turned, (values * weighting).astype(BF16)).astype(BF16)
            sent[micro * OWNERS : (micro + 1) * OWNERS, :, at] = state.reshape(OWNERS, OWNED, 128)
            grown = jnp.exp(each)
            growth[micro, :, at] = grown
            decay[micro, :, at] = grown[ROWS - 1 :, :]

    def decay_to(owner):
        return remote(
            decay.at[owner // OWNERS], decays.at[place], decay_s.at[owner], decay_r.at[place], {"seq": owner}
        )

    def state_to(owner):
        return remote(sent.at[owner], arrived.at[place], state_s.at[owner], state_r.at[place], {"seq": owner})

    def enter_to(owner):
        return remote(back.at[owner], entering.at[place], enter_s.at[owner], enter_r.at[place], {"seq": owner})

    def send_states(micro):
        for owner in range(micro * OWNERS, (micro + 1) * OWNERS):

            @pl.when(jnp.logical_and(place != owner, place < SEQ - 1))
            def _():
                decay_to(owner).start()
                state_to(owner).start()

    def gate(micro):
        raw = (dot(xg[micro], wg[...]) * scales[micro]).astype(BF16).astype(F32)
        gate_act[micro] = silu(raw)

    def inside(micro):
        cumulative, step_size = sums[micro], steps[micro]
        across_step, across_sum = step_size.T, cumulative.T
        scores = dot_turned(state_conv[micro, :, STATE:], state_conv[micro, :, 0:STATE])
        for pair in range(HEADS // 2):
            at = slice(pair * 128, pair * 128 + 128)
            values = inner_conv[micro, :, at]
            parts = []
            for h in (2 * pair, 2 * pair + 1):
                column = jnp.broadcast_to(cumulative[:, h : h + 1], (ROWS, 128))
                fade = jnp.exp(jnp.where(later, column - across_sum[h : h + 1, :], -jnp.inf))
                mixing = (scores * fade * across_step[h : h + 1, :]).astype(BF16)
                parts.append(dot(mixing, values))
            skips = [jnp.broadcast_to(skip_scale[:, h : h + 1], (1, 128)) for h in (2 * pair, 2 * pair + 1)]
            skip = jnp.where(first_half[0:1], skips[0], skips[1])
            mixed[micro, :, at] = jnp.where(first_half, parts[0], parts[1]) + skip * values.astype(F32)

    def scan():
        arrived[place] = sent[place]
        decays[place] = decay[place // OWNERS]
        carried = jnp.zeros((OWNED, LOCAL), F32)
        for source in range(SEQ):
            if source > 0:
                back[source] = carried.astype(BF16)

                @pl.when(place != source)
                def _():
                    enter_to(source).start()

            if source < SEQ - 1:

                @pl.when(place != source)
                def _():
                    remote(
                        sent.at[source], arrived.at[source], state_s.at[source], state_r.at[source], {"seq": source}
                    ).wait_recv()
                    remote(
                        decay.at[0], decays.at[source], decay_s.at[source], decay_r.at[source], {"seq": source}
                    ).wait_recv()

                carried = decays[source] * carried + arrived[source].astype(F32)

        @pl.when(place > 0)
        def _():
            entering[place] = back[place]

    def across(micro):
        for owner in range(micro * OWNERS, (micro + 1) * OWNERS):

            @pl.when(jnp.logical_and(place != owner, place > 0))
            def _():
                remote(
                    back.at[owner], entering.at[owner], enter_s.at[owner], enter_r.at[owner], {"seq": owner}
                ).wait_recv()

        from_state = state_conv[micro, :, STATE:]
        square = jnp.zeros((ROWS, 128), F32)
        for column in range(0, LOCAL, 128):
            at = slice(column, column + 128)
            entry = entering[micro * OWNERS : (micro + 1) * OWNERS, :, at].reshape(STATE, 128)
            value = mixed[micro, :, at] + growth[micro, :, at] * dot(from_state, entry)
            gated = value * gate_act[micro, :, at]
            square = square + gated * gated
            normed[micro, :, at] = (gated * inner_gain[:, at]).astype(BF16)
        return jnp.sum(square.T, axis=0, keepdims=True)

    spare_row = lax.broadcasted_iota(jnp.int32, (16, ROWS), 0)

    def split(total):
        high = total.astype(BF16).astype(F32)
        return jnp.where(spare_row < 8, high, total - high).astype(BF16)

    def half(micro, which):
        index = micro * CHIPS + which
        return remote(
            halves.at[micro, which, 1 - core], partner_half.at[micro, which], half_s.at[index], half_r.at[index],
            to_partner,
        )

    def spread(micro, total, which):
        at = pl.ds(pl.multiple_of(which * PAIR, 128), PAIR)
        product = dot(normed[micro], wo[:, at]).T
        spare = split(total)
        for side in range(2):
            halves[micro, which, side, 0:NARROW, :] = product[side * NARROW : (side + 1) * NARROW, :].astype(BF16)
            halves[micro, which, side, NARROW:SLAB, :] = spare
        half(micro, which).start()

    def unpacked(block):
        wide = block.astype(F32)
        return wide[0:NARROW], wide[NARROW : NARROW + 1] + wide[NARROW + 8 : NARROW + 9]

    def added(*terms):
        return tuple(sum(parts[1:], parts[0]) for parts in zip(*terms))

    def join(micro, which):
        half(micro, which).wait_recv()
        return added(unpacked(halves[micro, which, core]), unpacked(partner_half[micro, which]))

    def pack(micro, which, value):
        joined[micro, which, 0:NARROW, :] = value[0].astype(BF16)
        joined[micro, which, NARROW:SLAB, :] = split(value[1])

    def ways(micro):
        return (after, behind) if micro == 0 else (behind, after)

    def send_before(micro):
        through, _ = ways(micro)
        return remote(
            joined.at[micro, across_ring], before.at[micro], before_s.at[micro], before_r.at[micro], device(through)
        )

    def send_total(micro, way):
        which = ways(micro)[1 - way]
        index = micro * 2 + way
        return remote(
            joined.at[micro, which], totals.at[micro, way], total_s.at[index], total_r.at[index], device(which)
        )

    def spread_all(micro, total):
        through, direct = ways(micro)
        for which in (across_ring, direct, through, chip):
            spread(micro, total, which)

    def join_first(micro):
        _, direct = ways(micro)
        pack(micro, across_ring, join(micro, across_ring))
        send_before(micro).start()
        pack(micro, direct, join(micro, direct))
        send_total(micro, 0).start()

    def join_second(micro):
        through, _ = ways(micro)
        value = join(micro, through)
        send_before(micro).wait_recv()
        pack(micro, through, added(value, unpacked(before[micro])))
        send_total(micro, 1).start()

    def write(micro):
        return pltpu.make_async_copy(own.at[micro], out.at[0, micro], out_s.at[micro])

    def finish(micro):
        value = join(micro, chip)
        for way in range(2):
            send_total(micro, way).wait_recv()
            value = added(value, unpacked(totals[micro, way]))
        base = x[chip, micro, core].astype(F32)
        own[micro] = (base + value[0] * lax.rsqrt(value[1] / INNER + EPS)).astype(BF16)

        @pl.when(section == 0)
        def _():
            handover(micro).start()

        write(micro).start()

    scope = jax.named_scope
    with scope("own"):
        send_own(0)
        send_own(1)
    for load in loads[MICRO:12]:
        load.wait()
    with scope("near"):
        forward_near(0)
        project(0, chip, True)
        forward_near(1)
        project(1, chip, True)
    with scope("project"):
        project(0, after, False)
        project(0, behind, False)
        forward_far(0)
        project(1, after, False)
        project(1, behind, False)
        project(0, across_ring, False)
        project_end(0)
        forward_far(1)
        project(1, across_ring, False)
        project_end(1)
    with scope("states"):
        for micro in range(MICRO):
            states(micro)
            send_states(micro)
    with scope("fill"):
        for load in loads[12:]:
            load.wait()
        for micro in range(MICRO):
            gate(micro)
            inside(micro)
    with scope("scan"):
        scan()
    with scope("across0"):
        total = across(0)
    with scope("spread0"):
        spread_all(0, total)
    with scope("join0"):
        join_first(0)
    with scope("across1"):
        total = across(1)
    with scope("spread1"):
        spread_all(1, total)
    with scope("join1"):
        join_first(1)
    with scope("second"):
        join_second(0)
        join_second(1)
    with scope("finish"):
        finish(0)
        finish(1)

    for micro in range(MICRO):
        for send in range(SENDS):
            gather(micro, send).wait_send()
        for which in (across_ring, after, behind, chip):
            half(micro, which).wait_send()
        send_before(micro).wait_send()
        for way in range(2):
            send_total(micro, way).wait_send()

        @pl.when(place < SEQ - 1)
        def _():
            rim(micro).wait_send()

        @pl.when(section == 0)
        def _():
            handover(micro).wait_send()

        @pl.when(section == 1)
        def _():
            passing(micro).wait_send()

        write(micro).wait()

    for owner in range(SEQ):

        @pl.when(jnp.logical_and(place != owner, place < SEQ - 1))
        def _():
            decay_to(owner).wait_send()
            state_to(owner).wait_send()

        if owner > 0:

            @pl.when(place != owner)
            def _():
                enter_to(owner).wait_send()


def shards(
    tokens, pre_gain, gate_w, inner_w, state_w, step_w, inner_taps, state_taps, step_bias, decay_rate, skip_scale,
    inner_gain, out_w,
):
    hbm = pl.BlockSpec(memory_space=pltpu.HBM)
    dma = lambda count: pltpu.SemaphoreType.DMA((count,))
    result = pl.pallas_call(
        kernel,
        out_shape=jax.ShapeDtypeStruct((1, MICRO, NARROW, ROWS), BF16),
        in_specs=[hbm] * 13,
        out_specs=hbm,
        scratch_shapes=[
            pltpu.VMEM((CHIPS, MICRO, 2, NARROW, ROWS), BF16),
            pltpu.VMEM((MICRO, ROWS, WIDTH), BF16),
            pltpu.VMEM((WIDTH, BOTH), BF16),
            pltpu.VMEM((HEADS, WIDTH), BF16),
            pltpu.VMEM((WIDTH, LOCAL), BF16),
            pltpu.VMEM((LOCAL, WIDTH), BF16),
            pltpu.VMEM((1, WIDTH), F32),
            pltpu.VMEM((TAPS + 1, 1, LOCAL), F32),
            pltpu.VMEM((TAPS + 1, 1, 2 * STATE), F32),
            pltpu.VMEM((1, HEADS), F32),
            pltpu.VMEM((1, HEADS), F32),
            pltpu.VMEM((1, HEADS), F32),
            pltpu.VMEM((1, LOCAL), F32),
            pltpu.VMEM((MICRO, ROWS, BOTH), F32),
            pltpu.VMEM((MICRO, ROWS, HEADS), F32),
            pltpu.VMEM((MICRO, ROWS, LOCAL), F32),
            pltpu.VMEM((MICRO, ROWS, 128), F32),
            pltpu.VMEM((MICRO, ROWS, 1), F32),
            pltpu.VMEM((MICRO, EDGE + ROWS, BOTH), F32),
            pltpu.VMEM((MICRO, ROWS, LOCAL), BF16),
            pltpu.VMEM((MICRO, ROWS, 2 * STATE), BF16),
            pltpu.VMEM((MICRO, ROWS, 128), F32),
            pltpu.VMEM((MICRO, ROWS, 128), F32),
            pltpu.VMEM((MICRO, ROWS, LOCAL), F32),
            pltpu.VMEM((MICRO, ROWS, LOCAL), F32),
            pltpu.VMEM((MICRO, 1, LOCAL), F32),
            pltpu.VMEM((SEQ, 1, LOCAL), F32),
            pltpu.VMEM((SEQ, OWNED, LOCAL), BF16),
            pltpu.VMEM((SEQ, OWNED, LOCAL), BF16),
            pltpu.VMEM((SEQ, OWNED, LOCAL), BF16),
            pltpu.VMEM((SEQ, OWNED, LOCAL), BF16),
            pltpu.VMEM((MICRO, ROWS, LOCAL), BF16),
            pltpu.VMEM((MICRO, CHIPS, 2, SLAB, ROWS), BF16),
            pltpu.VMEM((MICRO, CHIPS, SLAB, ROWS), BF16),
            pltpu.VMEM((MICRO, CHIPS, SLAB, ROWS), BF16),
            pltpu.VMEM((MICRO, SLAB, ROWS), BF16),
            pltpu.VMEM((MICRO, 2, SLAB, ROWS), BF16),
            pltpu.VMEM((MICRO, NARROW, ROWS), BF16),
            pltpu.VMEM((MICRO, NARROW, ROWS), BF16),
            dma(14), dma(MICRO * SENDS), dma(SHARE * MICRO), dma(MICRO), dma(MICRO),
            dma(SEQ), dma(SEQ), dma(SEQ), dma(SEQ), dma(SEQ), dma(SEQ),
            dma(MICRO * CHIPS), dma(MICRO * CHIPS), dma(MICRO), dma(MICRO), dma(MICRO * 2), dma(MICRO * 2),
            dma(MICRO), dma(MICRO), dma(MICRO), dma(MICRO), dma(MICRO),
        ],
        compiler_params=pltpu.CompilerParams(
            collective_id=0, has_side_effects=True, vmem_limit_bytes=56 * 1024 * 1024
        ),
    )(
        jnp.swapaxes(tokens, 1, 2), pre_gain, gate_w, inner_w, state_w, jnp.swapaxes(step_w, 1, 2),
        jnp.swapaxes(inner_taps, 0, 1), jnp.swapaxes(state_taps, 0, 1), step_bias, decay_rate, skip_scale, inner_gain,
        out_w,
    )
    return jnp.swapaxes(result, 2, 3)


def solution(mesh):
    return jax.shard_map(
        shards,
        mesh=mesh,
        in_specs=(
            P(None, "seq", "tensor"),
            P("pipe", None),
            P("pipe", None, "tensor"),
            P("pipe", None, "tensor"),
            P("pipe", None, None),
            P("pipe", None, "tensor"),
            P("pipe", None, "tensor"),
            P("pipe", None, None),
            P("pipe", "tensor"),
            P("pipe", "tensor"),
            P("pipe", "tensor"),
            P("pipe", "tensor"),
            P("pipe", "tensor", None),
        ),
        out_specs=P("pipe", None, "seq", "tensor"),
        check_vma=False,
    )
```

time: 138 us -> 106 us (0.77)
  the two profiles are of different devices: /device:TPU:102 before, /device:TPU:6 now
where the time goes in v2:
time: 106 us; the launch traced here: 104 us
  Pallas kernels  102 us (96%)
  local copies, waits for them, and re-layouts  1.59 us (2%)
    pallas_call x1, Pallas kernels, shards(): pl.pallas_call(kernel, out_shape=jax.ShapeDtypeStruct((1, MICRO, NARROW,...  102 us

profile of v2, /device:TPU:6, one launch (start us, length us, event | category | flops | bytes accessed | tf_op | source)
XLA Modules:
  0.0 104.0 jit_solution(11707543771979682834)
XLA Ops:
  0.0 102.4 %shard_map.127 = bf16[1,2,320,128]{3,2,1,0:T(8,128)(2,1)} custom-call(bf16[2,320,128]{2,1,0:T(8,128)(2,1)} %bitcast.6, f32[1,2560]{1,0:T(1,128)} %pre_gain_h.1, bf16[1,2560,640]{2,1,0:T(8,128)(2,1)} %gate_h.1, bf16[1,2560,640]{2,1,0:T(8,128)(2,1)} %inner_h.1, bf16[1,2560,256]{2,1,0:T(8,128)(2,1)} %state_h.1, bf16[1,10,2560]{2,1,0:T(8,128)(2,1)} %bitcast.7, ...), custom_call_target="tpu_custom_call" | custom-call | tf_op jit(solution)/shard_map/pallas_call | solution.py:526
  102.4 1.6 %copy.15 = bf16[1,2,128,320]{2,3,1,0:T(8,128)(2,1)} copy(bf16[1,2,128,320]{2,3,1,0:T(8,128)(2,1)} %bitcast.5) | data formatting | bytes 327680

commit v3 on v2

v3 whole, which is shorter than its diff:
```python
import jax
import jax.numpy as jnp
from jax import lax
from jax.experimental import pallas as pl
from jax.experimental.pallas import tpu as pltpu
from jax.sharding import PartitionSpec as P

MESH = pl.DeviceIdType.MESH
F32, BF16 = jnp.float32, jnp.bfloat16
HIGHEST = lax.Precision.HIGHEST
EPS = 1e-05
SHARE, SEQ = 8, 16
CHIPS = SHARE // 2
MICRO, ROWS, WIDTH, INNER = 2, 128, 2560, 5120
NARROW = WIDTH // SHARE
PAIR = 2 * NARROW
LOCAL = INNER // SHARE
STATE = 128
BOTH = LOCAL + 2 * STATE
HEADS = 10
TAPS = 4
SLAB = NARROW + 16
OWNED = STATE // SEQ
EDGE = 8
HALF = NARROW // 2
SENDS = 10
EARLY, LATE = slice(0, HALF), slice(HALF, NARROW)
PARTS = (slice(0, HALF), slice(HALF, SLAB))


def silu(value):
    return value / (1.0 + jnp.exp(-value))


def dot(a, b, **options):
    return jnp.dot(a, b, preferred_element_type=F32, **options)


def dot_turned(a, b):
    return lax.dot_general(a, b, (((1,), (1,)), ((), ())), preferred_element_type=F32)


def remote(src, dst, send, recv, device):
    return pltpu.make_async_remote_copy(
        src_ref=src, dst_ref=dst, send_sem=send, recv_sem=recv, device_id=device, device_id_type=MESH
    )


def kernel(
    tokens, pre_gain_h, gate_h, inner_h, state_h, step_h, inner_taps_h, state_taps_h, bias_h, rate_h, skip_h, gain_h,
    out_h, out,
    x, xg, w1, wd, wg, wo, pre_gain, inner_taps, state_taps, bias, rate, skip_scale, inner_gain,
    acc, acc_d, gate_act, squares, scales, padded, inner_conv, state_conv, steps, sums, growth, mixed, decay, decays, sent,
    arrived, back, entering, normed, halves, partner_half, joined, before, totals, own,
    local_s, gather_s, gather_r, share_r, rim_s, rim_r, decay_s, decay_r, state_s, state_r, enter_s, enter_r, half_s, half_r,
    before_s, before_r, total_s, total_r, pipe_s, pipe_r,
):
    section, member, place = (lax.axis_index(name) for name in ("pipe", "tensor", "seq"))
    chip, core = member // 2, member % 2
    partner = member + 1 - 2 * core
    after, behind, across_ring = (lax.rem(chip + step, CHIPS) for step in (1, CHIPS - 1, 2))

    def device(which):
        return {"tensor": which * 2 + core}

    loads = [
        pltpu.make_async_copy(source, target, local_s.at[index])
        for index, (source, target) in enumerate(
            (
                (tokens.at[0], x.at[chip, 0, core]),
                (tokens.at[1], x.at[chip, 1, core]),
                (inner_h.at[0], w1.at[:, 0:LOCAL]),
                (state_h.at[0], w1.at[:, LOCAL:BOTH]),
                (step_h.at[0], wd),
                (pre_gain_h, pre_gain),
                (inner_taps_h, inner_taps),
                (state_taps_h, state_taps),
                (bias_h, bias),
                (rate_h, rate),
                (skip_h, skip_scale),
                (gain_h, inner_gain),
                (gate_h.at[0], wg),
                (out_h.at[0], wo),
            )
        )
    ]

    @pl.when(section == 0)
    def _():
        for load in loads[:MICRO]:
            load.start()

    for load in loads[MICRO:]:
        load.start()

    barrier = pltpu.get_barrier_semaphore()

    def greet(peer):
        pl.semaphore_signal(barrier, inc=1, device_id=peer, device_id_type=MESH)

    for step in range(1, SEQ):
        greet({"seq": lax.rem(place + step, SEQ)})
    greet({"pipe": 1 - section})
    greet(device(after))
    greet(device(behind))
    greet({"tensor": partner})

    steps[...] = jnp.zeros_like(steps)

    @pl.when(place == 0)
    def _():
        padded[:, 0:EDGE, :] = jnp.zeros((MICRO, EDGE, BOTH), F32)
        entering[...] = jnp.zeros_like(entering)

    pl.semaphore_wait(barrier, SEQ - 1 + 4)

    def handover(micro, part):
        index, rows = micro * 2 + part, (EARLY, LATE)[part]
        return remote(
            own.at[micro, rows], x.at[chip, micro, core, rows], pipe_s.at[index], pipe_r.at[index], {"pipe": 1}
        )

    to_partner = {"tensor": partner}

    def gather(micro, send):
        which, part, target = (
            (chip, 0, after),
            (chip, 1, behind),
            (chip, 1, after),
            (chip, 0, behind),
            (behind, 0, after),
            (after, 1, behind),
            (chip, 2, None),
            (behind, 2, None),
            (after, 2, None),
            (across_ring, 2, None),
        )[send]
        send_sem = gather_s.at[micro * SENDS + send]
        if part == 2:
            block = x.at[which, micro, core]
            return remote(block, block, send_sem, share_r.at[which * MICRO + micro], to_partner)
        block = x.at[which, micro, core, (EARLY, LATE)[part]]
        return remote(block, block, send_sem, gather_r.at[(which * MICRO + micro) * 2 + part], device(target))

    def arrival(micro, which, part):
        block = x.at[which, micro, core, (EARLY, LATE)[part]]
        index = (which * MICRO + micro) * 2 + part
        return remote(block, block, gather_s.at[micro * SENDS], gather_r.at[index], to_partner)

    def shared(micro, which):
        block = x.at[which, micro, 1 - core]
        return remote(block, block, gather_s.at[micro * SENDS], share_r.at[which * MICRO + micro], to_partner)

    def start_own(micro):
        for send in (0, 1, 2, 3, 6):
            gather(micro, send).start()

    def send_loaded(micro):
        @pl.when(section == 0)
        def _():
            loads[micro].wait()
            start_own(micro)

    def send_passed(micro):
        @pl.when(section == 1)
        def _():
            for part in range(2):
                handover(micro, part).wait_recv()
            start_own(micro)

    def forward_near(micro):
        arrival(micro, behind, 0).wait_recv()
        gather(micro, 4).start()
        arrival(micro, after, 1).wait_recv()
        gather(micro, 5).start()
        arrival(micro, behind, 1).wait_recv()
        gather(micro, 7).start()
        arrival(micro, after, 0).wait_recv()
        gather(micro, 8).start()

    def forward_far(micro):
        arrival(micro, across_ring, 0).wait_recv()
        arrival(micro, across_ring, 1).wait_recv()
        gather(micro, 9).start()

    def project(micro, which, first):
        shared(micro, which).wait_recv()
        wide = x[which, micro].reshape(PAIR, ROWS).astype(F32).T
        at = pl.ds(pl.multiple_of(which * PAIR, 128), PAIR)
        scaled = (wide * pre_gain[:, at]).astype(BF16)
        xg[micro, :, at] = scaled
        square = wide * wide
        square = sum(square[:, column : column + 128] for column in range(0, PAIR, 128))
        term = dot(scaled, w1[at, :])
        term_d = dot_turned(scaled, wd[:, at])
        if first:
            acc[micro], acc_d[micro], squares[micro] = term, term_d, square
        else:
            acc[micro] += term
            acc_d[micro] += term_d
            squares[micro] += square

    def rim(micro):
        return remote(
            padded.at[micro, ROWS : ROWS + EDGE, :], padded.at[micro, 0:EDGE, :], rim_s.at[micro], rim_r.at[micro],
            {"seq": lax.rem(place + 1, SEQ)},
        )

    def project_end(micro):
        scale = lax.rsqrt(jnp.sum(squares[micro], axis=1, keepdims=True) / WIDTH + EPS)
        scales[micro] = scale
        padded[micro, EDGE : EDGE + ROWS, :] = (acc[micro] * scale).astype(BF16).astype(F32)

        @pl.when(place < SEQ - 1)
        def _():
            rim(micro).start()

        shifted = acc_d[micro] * scale + bias[...]
        steps[micro, :, 0:HEADS] = jnp.maximum(shifted, 0.0) + jnp.log1p(jnp.exp(-jnp.abs(shifted)))

    row = lax.broadcasted_iota(jnp.int32, (ROWS, ROWS), 0)
    lane = lax.broadcasted_iota(jnp.int32, (ROWS, ROWS), 1)
    first_half = lane < 64
    later = row >= lane

    def states(micro):
        rates = jnp.concatenate([rate[...], jnp.zeros((1, 128 - HEADS), F32)], axis=1)
        step_size = steps[micro]
        cumulative = dot(later.astype(F32), -step_size * rates, precision=HIGHEST)
        sums[micro] = cumulative
        decay[micro] = jnp.exp(cumulative[ROWS - 1 :, :])

        @pl.when(place > 0)
        def _():
            rim(micro).wait_recv()

        for column in range(0, BOTH, 128):
            taps, at = (inner_taps, column) if column < LOCAL else (state_taps, column - LOCAL)
            total = jnp.broadcast_to(taps[TAPS, :, at : at + 128], (ROWS, 128))
            for index in range(TAPS):
                begin = EDGE - TAPS + 1 + index
                total = total + taps[index, :, at : at + 128] * (
                    padded[micro, begin : begin + ROWS, column : column + 128]
                )
            result = silu(total).astype(BF16)
            if column < LOCAL:
                inner_conv[micro, :, at : at + 128] = result
            else:
                state_conv[micro, :, at : at + 128] = result

        turned = state_conv[micro, :, 0:STATE].astype(F32).T.astype(BF16)
        for pair in range(HEADS // 2):
            heads = (2 * pair, 2 * pair + 1)
            at = slice(pair * 128, pair * 128 + 128)
            spread = [jnp.broadcast_to(cumulative[:, h : h + 1], (ROWS, 128)) for h in heads]
            sizes = [jnp.broadcast_to(step_size[:, h : h + 1], (ROWS, 128)) for h in heads]
            each = jnp.where(first_half, spread[0], spread[1])
            values = inner_conv[micro, :, at].astype(F32)
            weighting = jnp.exp(each[ROWS - 1 :, :] - each) * jnp.where(first_half, sizes[0], sizes[1])
            state = dot(turned, (values * weighting).astype(BF16))
            sent[micro, :, :, at] = state.reshape(SEQ, OWNED, 128).astype(BF16)
            growth[micro, :, at] = jnp.exp(each)

    distances = (4, 3, 5, 2, 6, 1, 7, 0)
    others = [
        lax.rem(place // 2 + step, SEQ // 2) * 2 + side
        for step in distances
        for side in range(2)
    ]

    def decay_to(micro, owner):
        index = micro * SEQ
        return remote(
            decay.at[micro], decays.at[micro, place], decay_s.at[index + owner], decay_r.at[index + place],
            {"seq": owner},
        )

    def state_to(micro, owner):
        index = micro * SEQ
        return remote(
            sent.at[micro, owner], arrived.at[micro, place], state_s.at[index + owner], state_r.at[index + place],
            {"seq": owner},
        )

    def enter_to(micro, target):
        index = micro * SEQ
        return remote(
            back.at[micro, target], entering.at[micro, place], enter_s.at[index + target], enter_r.at[index + place],
            {"seq": target},
        )

    def incoming(micro, source):
        index = micro * SEQ + source
        to = {"seq": source}
        return (
            remote(decay.at[micro], decays.at[micro, source], decay_s.at[index], decay_r.at[index], to),
            remote(sent.at[micro, source], arrived.at[micro, source], state_s.at[index], state_r.at[index], to),
        )

    def send_states(micro):
        for owner in others:

            @pl.when(jnp.logical_and(place != owner, place < SEQ - 1))
            def _():
                decay_to(micro, owner).start()
                state_to(micro, owner).start()

    def gate(micro):
        raw = (dot(xg[micro], wg[...]) * scales[micro]).astype(BF16).astype(F32)
        gate_act[micro] = silu(raw)

    def inside(micro):
        cumulative, step_size = sums[micro], steps[micro]
        across_step, across_sum = step_size.T, cumulative.T
        scores = dot_turned(state_conv[micro, :, STATE:], state_conv[micro, :, 0:STATE])
        for pair in range(HEADS // 2):
            at = slice(pair * 128, pair * 128 + 128)
            values = inner_conv[micro, :, at]
            parts = []
            for h in (2 * pair, 2 * pair + 1):
                column = jnp.broadcast_to(cumulative[:, h : h + 1], (ROWS, 128))
                fade = jnp.exp(jnp.where(later, column - across_sum[h : h + 1, :], -jnp.inf))
                mixing = (scores * fade * across_step[h : h + 1, :]).astype(BF16)
                parts.append(dot(mixing, values))
            skips = [jnp.broadcast_to(skip_scale[:, h : h + 1], (1, 128)) for h in (2 * pair, 2 * pair + 1)]
            skip = jnp.where(first_half[0:1], skips[0], skips[1])
            mixed[micro, :, at] = jnp.where(first_half, parts[0], parts[1]) + skip * values.astype(F32)

    head_of = lax.broadcasted_iota(jnp.int32, (128, LOCAL), 1) // 64
    expand = (head_of == lax.broadcasted_iota(jnp.int32, (128, LOCAL), 0)).astype(F32)

    def scan(micro):
        arrived[micro, place] = sent[micro, place]
        decays[micro, place] = decay[micro]
        for source in range(SEQ - 1):

            @pl.when(place != source)
            def _():
                for copy in incoming(micro, source):
                    copy.wait_recv()

        rows = jnp.concatenate([decays[micro, source] for source in range(SEQ)], axis=0)
        factors = dot(rows, expand, precision=HIGHEST)
        carried = jnp.zeros((OWNED, LOCAL), F32)
        for source in range(SEQ - 1):
            carried = factors[source : source + 1, :] * carried + arrived[micro, source].astype(F32)
            back[micro, source + 1] = carried.astype(BF16)

        for target in others:

            @pl.when(jnp.logical_and(place != target, target > 0))
            def _():
                enter_to(micro, target).start()

        @pl.when(place > 0)
        def _():
            entering[micro, place] = back[micro, place]

    def across(micro):
        for owner in range(SEQ):

            @pl.when(jnp.logical_and(place != owner, place > 0))
            def _():
                index = micro * SEQ + owner
                remote(
                    back.at[micro, owner], entering.at[micro, owner], enter_s.at[index], enter_r.at[index],
                    {"seq": owner},
                ).wait_recv()

        from_state = state_conv[micro, :, STATE:]
        square = jnp.zeros((ROWS, 128), F32)
        for column in range(0, LOCAL, 128):
            at = slice(column, column + 128)
            entry = entering[micro, :, :, at].astype(F32).reshape(STATE, 128).astype(BF16)
            value = mixed[micro, :, at] + growth[micro, :, at] * dot(from_state, entry)
            gated = value * gate_act[micro, :, at]
            square = square + gated * gated
            normed[micro, :, at] = (gated * inner_gain[:, at]).astype(BF16)
        return jnp.sum(square.T, axis=0, keepdims=True)

    spare_row = lax.broadcasted_iota(jnp.int32, (16, ROWS), 0)

    def split(total):
        high = total.astype(BF16).astype(F32)
        return jnp.where(spare_row < 8, high, total - high).astype(BF16)

    def half(micro, which):
        index = micro * CHIPS + which
        return remote(
            halves.at[micro, which, 1 - core], partner_half.at[micro, which], half_s.at[index], half_r.at[index],
            to_partner,
        )

    def spread(micro, total, which):
        at = pl.ds(pl.multiple_of(which * PAIR, 128), PAIR)
        product = dot(normed[micro], wo[:, at]).T
        spare = split(total)
        for side in range(2):
            halves[micro, which, side, 0:NARROW, :] = product[side * NARROW : (side + 1) * NARROW, :].astype(BF16)
            halves[micro, which, side, NARROW:SLAB, :] = spare
        half(micro, which).start()

    def unpacked(block, part):
        wide = block.astype(F32)
        if part == 0:
            return (wide,)
        rest = NARROW - HALF
        return wide[0:rest], wide[rest : rest + 1] + wide[rest + 8 : rest + 9]

    def added(*terms):
        return tuple(sum(values[1:], values[0]) for values in zip(*terms))

    def join(micro, which, part):
        rows = PARTS[part]
        return added(
            unpacked(halves[micro, which, core, rows], part), unpacked(partner_half[micro, which, rows], part)
        )

    def pack(micro, which, part, value):
        if part == 0:
            joined[micro, which, EARLY, :] = value[0].astype(BF16)
        else:
            joined[micro, which, LATE, :] = value[0].astype(BF16)
            joined[micro, which, NARROW:SLAB, :] = split(value[1])

    ways = (after, behind)

    def send_before(micro, part):
        rows, index = PARTS[part], micro * 2 + part
        return remote(
            joined.at[micro, across_ring, rows], before.at[micro, rows], before_s.at[index], before_r.at[index],
            device(ways[part]),
        )

    def send_total(micro, way, part):
        rows, index = PARTS[part], (micro * 2 + way) * 2 + part
        return remote(
            joined.at[micro, ways[way], rows], totals.at[micro, way, rows], total_s.at[index], total_r.at[index],
            device(ways[way]),
        )

    def join_before(micro):
        half(micro, across_ring).wait_recv()
        for part in range(2):
            pack(micro, across_ring, part, join(micro, across_ring, part))
            send_before(micro, part).start()

    def join_direct(micro, way):
        which, part = ways[way], 1 - way
        half(micro, which).wait_recv()
        pack(micro, which, part, join(micro, which, part))
        send_total(micro, way, part).start()

    def join_second(micro):
        for part in range(2):
            which = ways[part]
            value = join(micro, which, part)
            send_before(micro, part).wait_recv()
            pack(micro, which, part, added(value, unpacked(before[micro, PARTS[part]], part)))
            send_total(micro, part, part).start()

    def finish(micro):
        half(micro, chip).wait_recv()
        values = [join(micro, chip, part) for part in range(2)]
        for way, part in ((0, 1), (1, 0), (0, 0), (1, 1)):
            send_total(micro, way, part).wait_recv()
            values[part] = added(values[part], unpacked(totals[micro, way, PARTS[part]], part))
        scale = lax.rsqrt(values[1][1] / INNER + EPS)
        for part, rows in enumerate((EARLY, LATE)):
            result = (x[chip, micro, core, rows].astype(F32) + values[part][0] * scale).astype(BF16)
            own[micro, rows] = result
            out[0, micro, rows] = result

            @pl.when(section == 0)
            def _():
                handover(micro, part).start()

    scope = jax.named_scope
    with scope("own"):
        send_loaded(0)
        send_loaded(1)
        send_passed(0)
    for load in loads[MICRO:12]:
        load.wait()
    with scope("near0"):
        forward_near(0)
    with scope("p0"):
        project(0, chip, True)
        project(0, behind, False)
        project(0, after, False)
    with scope("far0"):
        forward_far(0)
        project(0, across_ring, False)
        project_end(0)
    with scope("own1"):
        send_passed(1)
    with scope("near1"):
        forward_near(1)
    with scope("p1"):
        project(1, chip, True)
        project(1, behind, False)
        project(1, after, False)
    with scope("states0"):
        states(0)
        send_states(0)
    with scope("far1"):
        forward_far(1)
        project(1, across_ring, False)
        project_end(1)
    for load in loads[12:]:
        load.wait()
    with scope("fill0"):
        gate(0)
        inside(0)
    with scope("states1"):
        states(1)
        send_states(1)
    with scope("fill1"):
        gate(1)
        inside(1)
    with scope("scan0"):
        scan(0)
    with scope("scan1"):
        scan(1)
    with scope("across0"):
        total = across(0)
    with scope("spread0"):
        spread(0, total, across_ring)
        spread(0, total, after)
        spread(0, total, behind)
        join_before(0)
    with scope("across1"):
        total1 = across(1)
    with scope("spread1"):
        spread(1, total1, across_ring)
        join_direct(0, 0)
        spread(1, total1, after)
        join_direct(0, 1)
        join_before(1)
        spread(0, total, chip)
    with scope("second0"):
        join_second(0)
        spread(1, total1, behind)
        join_direct(1, 0)
        spread(1, total1, chip)
        join_direct(1, 1)
    with scope("finish0"):
        finish(0)
    with scope("sent"):
        for micro in range(MICRO):
            for send in range(SENDS):
                gather(micro, send).wait_send()

            @pl.when(place < SEQ - 1)
            def _():
                rim(micro).wait_send()

            for owner in range(SEQ):

                @pl.when(jnp.logical_and(place != owner, place < SEQ - 1))
                def _():
                    decay_to(micro, owner).wait_send()
                    state_to(micro, owner).wait_send()

                if owner > 0:

                    @pl.when(place != owner)
                    def _():
                        enter_to(micro, owner).wait_send()

    with scope("second1"):
        join_second(1)
    with scope("finish1"):
        finish(1)

    for micro in range(MICRO):
        for which in (across_ring, after, behind, chip):
            half(micro, which).wait_send()
        for part in range(2):
            send_before(micro, part).wait_send()
            for way in range(2):
                send_total(micro, way, part).wait_send()

        @pl.when(section == 0)
        def _():
            for part in range(2):
                handover(micro, part).wait_send()


def shards(
    tokens, pre_gain, gate_w, inner_w, state_w, step_w, inner_taps, state_taps, step_bias, decay_rate, skip_scale,
    inner_gain, out_w,
):
    hbm = pl.BlockSpec(memory_space=pltpu.HBM)
    dma = lambda count: pltpu.SemaphoreType.DMA((count,))
    result = pl.pallas_call(
        kernel,
        out_shape=pltpu.VMEM((1, MICRO, NARROW, ROWS), BF16),
        in_specs=[hbm] * 13,
        out_specs=pl.BlockSpec(memory_space=pltpu.VMEM),
        scratch_shapes=[
            pltpu.VMEM((CHIPS, MICRO, 2, NARROW, ROWS), BF16),
            pltpu.VMEM((MICRO, ROWS, WIDTH), BF16),
            pltpu.VMEM((WIDTH, BOTH), BF16),
            pltpu.VMEM((HEADS, WIDTH), BF16),
            pltpu.VMEM((WIDTH, LOCAL), BF16),
            pltpu.VMEM((LOCAL, WIDTH), BF16),
            pltpu.VMEM((1, WIDTH), F32),
            pltpu.VMEM((TAPS + 1, 1, LOCAL), F32),
            pltpu.VMEM((TAPS + 1, 1, 2 * STATE), F32),
            pltpu.VMEM((1, HEADS), F32),
            pltpu.VMEM((1, HEADS), F32),
            pltpu.VMEM((1, HEADS), F32),
            pltpu.VMEM((1, LOCAL), F32),
            pltpu.VMEM((MICRO, ROWS, BOTH), F32),
            pltpu.VMEM((MICRO, ROWS, HEADS), F32),
            pltpu.VMEM((MICRO, ROWS, LOCAL), F32),
            pltpu.VMEM((MICRO, ROWS, 128), F32),
            pltpu.VMEM((MICRO, ROWS, 1), F32),
            pltpu.VMEM((MICRO, EDGE + ROWS, BOTH), F32),
            pltpu.VMEM((MICRO, ROWS, LOCAL), BF16),
            pltpu.VMEM((MICRO, ROWS, 2 * STATE), BF16),
            pltpu.VMEM((MICRO, ROWS, 128), F32),
            pltpu.VMEM((MICRO, ROWS, 128), F32),
            pltpu.VMEM((MICRO, ROWS, LOCAL), F32),
            pltpu.VMEM((MICRO, ROWS, LOCAL), F32),
            pltpu.VMEM((MICRO, 1, 128), F32),
            pltpu.VMEM((MICRO, SEQ, 1, 128), F32),
            pltpu.VMEM((MICRO, SEQ, OWNED, LOCAL), BF16),
            pltpu.VMEM((MICRO, SEQ, OWNED, LOCAL), BF16),
            pltpu.VMEM((MICRO, SEQ, OWNED, LOCAL), BF16),
            pltpu.VMEM((MICRO, SEQ, OWNED, LOCAL), BF16),
            pltpu.VMEM((MICRO, ROWS, LOCAL), BF16),
            pltpu.VMEM((MICRO, CHIPS, 2, SLAB, ROWS), BF16),
            pltpu.VMEM((MICRO, CHIPS, SLAB, ROWS), BF16),
            pltpu.VMEM((MICRO, CHIPS, SLAB, ROWS), BF16),
            pltpu.VMEM((MICRO, SLAB, ROWS), BF16),
            pltpu.VMEM((MICRO, 2, SLAB, ROWS), BF16),
            pltpu.VMEM((MICRO, NARROW, ROWS), BF16),
            dma(14), dma(MICRO * SENDS), dma(CHIPS * MICRO * 2), dma(CHIPS * MICRO), dma(MICRO), dma(MICRO),
            dma(MICRO * SEQ), dma(MICRO * SEQ), dma(MICRO * SEQ), dma(MICRO * SEQ), dma(MICRO * SEQ), dma(MICRO * SEQ),
            dma(MICRO * CHIPS), dma(MICRO * CHIPS), dma(MICRO * 2), dma(MICRO * 2), dma(MICRO * 4), dma(MICRO * 4),
            dma(MICRO * 2), dma(MICRO * 2),
        ],
        compiler_params=pltpu.CompilerParams(
            collective_id=0, has_side_effects=True, vmem_limit_bytes=56 * 1024 * 1024
        ),
    )(
        jnp.swapaxes(tokens, 1, 2), pre_gain, gate_w, inner_w, state_w, jnp.swapaxes(step_w, 1, 2),
        jnp.swapaxes(inner_taps, 0, 1), jnp.swapaxes(state_taps, 0, 1), step_bias, decay_rate, skip_scale, inner_gain,
        out_w,
    )
    return jnp.swapaxes(result, 2, 3)


def solution(mesh):
    return jax.shard_map(
        shards,
        mesh=mesh,
        in_specs=(
            P(None, "seq", "tensor"),
            P("pipe", None),
            P("pipe", None, "tensor"),
            P("pipe", None, "tensor"),
            P("pipe", None, None),
            P("pipe", None, "tensor"),
            P("pipe", None, "tensor"),
            P("pipe", None, None),
            P("pipe", "tensor"),
            P("pipe", "tensor"),
            P("pipe", "tensor"),
            P("pipe", "tensor"),
            P("pipe", "tensor", None),
        ),
        out_specs=P("pipe", None, "seq", "tensor"),
        check_vma=False,
    )
```

time: 106 us -> 103 us (0.972); the launches traced: 104 us -> 103 us
  no operation moved by 1% of the time
where the time goes in v3:
time: 103 us
  Pallas kernels  102 us (99%)
    pallas_call x1, Pallas kernels, shards(): pl.pallas_call(kernel, out_shape=pltpu.VMEM((1, MICRO, NARROW, ROWS), BF1...  102 us

profile of v3, /device:TPU:6, one launch (start us, length us, event | category | flops | bytes accessed | tf_op | source)
XLA Modules:
  0.0 103.0 jit_solution(14733450295025775734)
XLA Ops:
  0.0 102.3 %shard_map.127 = bf16[1,2,320,128]{3,2,1,0:T(8,128)(2,1)S(1)} custom-call(bf16[2,320,128]{2,1,0:T(8,128)(2,1)} %bitcast.6, f32[1,2560]{1,0:T(1,128)} %pre_gain_h.1, bf16[1,2560,640]{2,1,0:T(8,128)(2,1)} %gate_h.1, bf16[1,2560,640]{2,1,0:T(8,128)(2,1)} %inner_h.1, bf16[1,2560,256]{2,1,0:T(8,128)(2,1)} %state_h.1, bf16[1,10,2560]{2,1,0:T(8,128)(2,1)} %bitcast.7, ...), custom_call_target="tpu_custom_call" | custom-call | tf_op jit(solution)/shard_map/pallas_call | solution.py:596
  102.4 0.7 copy.15

commit v4 on v3

--- a/solution.py
+++ b/solution.py
@@ -24,6 +24,7 @@
 EDGE = 8
 HALF = NARROW // 2
 SENDS = 10
+NEAR = 4
 EARLY, LATE = slice(0, HALF), slice(HALF, NARROW)
 PARTS = (slice(0, HALF), slice(HALF, SLAB))
 
@@ -115,10 +116,13 @@
     pl.semaphore_wait(barrier, SEQ - 1 + 4)
 
     def handover(micro, part):
-        index, rows = micro * 2 + part, (EARLY, LATE)[part]
-        return remote(
-            own.at[micro, rows], x.at[chip, micro, core, rows], pipe_s.at[index], pipe_r.at[index], {"pipe": 1}
-        )
+        rows = (EARLY, LATE)[part]
+        return remote(
+            own.at[micro, rows], x.at[chip, micro, core, rows], pipe_s.at[0], pipe_r.at[micro], {"pipe": 1}
+        )
+
+    def handed_over(micro):
+        return remote(own.at[micro], x.at[chip, micro, core], pipe_s.at[0], pipe_r.at[micro], {"pipe": 1})
 
     to_partner = {"tensor": partner}
 
@@ -135,21 +139,24 @@
             (after, 2, None),
             (across_ring, 2, None),
         )[send]
-        send_sem = gather_s.at[micro * SENDS + send]
         if part == 2:
             block = x.at[which, micro, core]
-            return remote(block, block, send_sem, share_r.at[which * MICRO + micro], to_partner)
+            return remote(block, block, gather_s.at[1], share_r.at[which * MICRO + micro], to_partner)
         block = x.at[which, micro, core, (EARLY, LATE)[part]]
-        return remote(block, block, send_sem, gather_r.at[(which * MICRO + micro) * 2 + part], device(target))
-
-    def arrival(micro, which, part):
+        slot = NEAR * MICRO + micro if send in (4, 5) else micro * NEAR + (0, 3, 1, 2)[send]
+        return remote(block, block, gather_s.at[0], gather_r.at[slot], device(target))
+
+    def near(micro, which, part, slot):
         block = x.at[which, micro, core, (EARLY, LATE)[part]]
-        index = (which * MICRO + micro) * 2 + part
-        return remote(block, block, gather_s.at[micro * SENDS], gather_r.at[index], to_partner)
+        return remote(block, block, gather_s.at[0], gather_r.at[micro * NEAR + slot], to_partner)
+
+    def far(micro):
+        block = x.at[across_ring, micro, core]
+        return remote(block, block, gather_s.at[0], gather_r.at[NEAR * MICRO + micro], to_partner)
 
     def shared(micro, which):
         block = x.at[which, micro, 1 - core]
-        return remote(block, block, gather_s.at[micro * SENDS], share_r.at[which * MICRO + micro], to_partner)
+        return remote(block, block, gather_s.at[1], share_r.at[which * MICRO + micro], to_partner)
 
     def start_own(micro):
         for send in (0, 1, 2, 3, 6):
@@ -164,23 +171,21 @@
     def send_passed(micro):
         @pl.when(section == 1)
         def _():
-            for part in range(2):
-                handover(micro, part).wait_recv()
+            handed_over(micro).wait_recv()
             start_own(micro)
 
     def forward_near(micro):
-        arrival(micro, behind, 0).wait_recv()
+        near(micro, behind, 0, 0).wait_recv()
         gather(micro, 4).start()
-        arrival(micro, after, 1).wait_recv()
+        near(micro, after, 1, 3).wait_recv()
         gather(micro, 5).start()
-        arrival(micro, behind, 1).wait_recv()
+        near(micro, behind, 1, 1).wait_recv()
         gather(micro, 7).start()
-        arrival(micro, after, 0).wait_recv()
+        near(micro, after, 0, 2).wait_recv()
         gather(micro, 8).start()
 
     def forward_far(micro):
-        arrival(micro, across_ring, 0).wait_recv()
-        arrival(micro, across_ring, 1).wait_recv()
+        far(micro).wait_recv()
         gather(micro, 9).start()
 
     def project(micro, which, first):
@@ -269,33 +274,31 @@
     ]
 
     def decay_to(micro, owner):
-        index = micro * SEQ
-        return remote(
-            decay.at[micro], decays.at[micro, place], decay_s.at[index + owner], decay_r.at[index + place],
-            {"seq": owner},
+        return remote(
+            decay.at[micro], decays.at[micro, place], decay_s.at[micro], decay_r.at[micro], {"seq": owner}
         )
 
     def state_to(micro, owner):
-        index = micro * SEQ
-        return remote(
-            sent.at[micro, owner], arrived.at[micro, place], state_s.at[index + owner], state_r.at[index + place],
-            {"seq": owner},
+        return remote(
+            sent.at[micro, owner], arrived.at[micro, place], state_s.at[micro], state_r.at[micro], {"seq": owner}
         )
 
     def enter_to(micro, target):
-        index = micro * SEQ
-        return remote(
-            back.at[micro, target], entering.at[micro, place], enter_s.at[index + target], enter_r.at[index + place],
-            {"seq": target},
-        )
-
-    def incoming(micro, source):
-        index = micro * SEQ + source
-        to = {"seq": source}
-        return (
-            remote(decay.at[micro], decays.at[micro, source], decay_s.at[index], decay_r.at[index], to),
-            remote(sent.at[micro, source], arrived.at[micro, source], state_s.at[index], state_r.at[index], to),
-        )
+        return remote(
+            back.at[micro, target], entering.at[micro, place], enter_s.at[micro], enter_r.at[micro], {"seq": target}
+        )
+
+    def all_decays(micro, count):
+        block = decays.at[micro, 0:count]
+        return remote(block, block, decay_s.at[micro], decay_r.at[micro], to_partner)
+
+    def all_states(micro, count):
+        block = arrived.at[micro, 0:count]
+        return remote(block, block, state_s.at[micro], state_r.at[micro], to_partner)
+
+    def all_entering(micro, count):
+        block = entering.at[micro, 0:count]
+        return remote(block, block, enter_s.at[micro], enter_r.at[micro], to_partner)
 
     def send_states(micro):
         for owner in others:
@@ -332,12 +335,15 @@
     def scan(micro):
         arrived[micro, place] = sent[micro, place]
         decays[micro, place] = decay[micro]
-        for source in range(SEQ - 1):
-
-            @pl.when(place != source)
-            def _():
-                for copy in incoming(micro, source):
-                    copy.wait_recv()
+        @pl.when(place < SEQ - 1)
+        def _():
+            all_decays(micro, SEQ - 2).wait_recv()
+            all_states(micro, SEQ - 2).wait_recv()
+
+        @pl.when(place == SEQ - 1)
+        def _():
+            all_decays(micro, SEQ - 1).wait_recv()
+            all_states(micro, SEQ - 1).wait_recv()
 
         rows = jnp.concatenate([decays[micro, source] for source in range(SEQ)], axis=0)
         factors = dot(rows, expand, precision=HIGHEST)
@@ -357,15 +363,9 @@
             entering[micro, place] = back[micro, place]
 
     def across(micro):
-        for owner in range(SEQ):
-
-            @pl.when(jnp.logical_and(place != owner, place > 0))
-            def _():
-                index = micro * SEQ + owner
-                remote(
-                    back.at[micro, owner], entering.at[micro, owner], enter_s.at[index], enter_r.at[index],
-                    {"seq": owner},
-                ).wait_recv()
+        @pl.when(place > 0)
+        def _():
+            all_entering(micro, SEQ - 1).wait_recv()
 
         from_state = state_conv[micro, :, STATE:]
         square = jnp.zeros((ROWS, 128), F32)
@@ -387,7 +387,7 @@
     def half(micro, which):
         index = micro * CHIPS + which
         return remote(
-            halves.at[micro, which, 1 - core], partner_half.at[micro, which], half_s.at[index], half_r.at[index],
+            halves.at[micro, which, 1 - core], partner_half.at[micro, which], half_s.at[0], half_r.at[index],
             to_partner,
         )
 
@@ -428,16 +428,19 @@
     def send_before(micro, part):
         rows, index = PARTS[part], micro * 2 + part
         return remote(
-            joined.at[micro, across_ring, rows], before.at[micro, rows], before_s.at[index], before_r.at[index],
+            joined.at[micro, across_ring, rows], before.at[micro, rows], before_s.at[0], before_r.at[index],
             device(ways[part]),
         )
 
     def send_total(micro, way, part):
-        rows, index = PARTS[part], (micro * 2 + way) * 2 + part
-        return remote(
-            joined.at[micro, ways[way], rows], totals.at[micro, way, rows], total_s.at[index], total_r.at[index],
+        rows = PARTS[part]
+        return remote(
+            joined.at[micro, ways[way], rows], totals.at[micro, way, rows], total_s.at[0], total_r.at[micro],
             device(ways[way]),
         )
+
+    def every(block, send, recv):
+        return remote(block, block, send, recv, to_partner)
 
     def join_before(micro):
         half(micro, across_ring).wait_recv()
@@ -462,8 +465,8 @@
     def finish(micro):
         half(micro, chip).wait_recv()
         values = [join(micro, chip, part) for part in range(2)]
+        every(totals.at[micro], total_s.at[0], total_r.at[micro]).wait_recv()
         for way, part in ((0, 1), (1, 0), (0, 0), (1, 1)):
-            send_total(micro, way, part).wait_recv()
             values[part] = added(values[part], unpacked(totals[micro, way, PARTS[part]], part))
         scale = lax.rsqrt(values[1][1] / INNER + EPS)
         for part, rows in enumerate((EARLY, LATE)):
@@ -487,15 +490,23 @@
     with scope("p0"):
         project(0, chip, True)
         project(0, behind, False)
+    with scope("own1"):
+        send_passed(1)
         project(0, after, False)
+
+    @pl.when(section == 0)
+    def _():
+        forward_near(1)
+
     with scope("far0"):
         forward_far(0)
         project(0, across_ring, False)
         project_end(0)
-    with scope("own1"):
-        send_passed(1)
-    with scope("near1"):
+
+    @pl.when(section == 1)
+    def _():
         forward_near(1)
+
     with scope("p1"):
         project(1, chip, True)
         project(1, behind, False)
@@ -547,44 +558,36 @@
     with scope("finish0"):
         finish(0)
     with scope("sent"):
+        every(x.at[0:3, 0], gather_s.at[0], share_r.at[0]).wait_send()
+        every(x.at[0:2], gather_s.at[1], share_r.at[0]).wait_send()
         for micro in range(MICRO):
-            for send in range(SENDS):
-                gather(micro, send).wait_send()
 
             @pl.when(place < SEQ - 1)
             def _():
                 rim(micro).wait_send()
-
-            for owner in range(SEQ):
-
-                @pl.when(jnp.logical_and(place != owner, place < SEQ - 1))
-                def _():
-                    decay_to(micro, owner).wait_send()
-                    state_to(micro, owner).wait_send()
-
-                if owner > 0:
-
-                    @pl.when(place != owner)
-                    def _():
-                        enter_to(micro, owner).wait_send()
+                all_decays(micro, SEQ - 1).wait_send()
+                all_states(micro, SEQ - 1).wait_send()
+
+            @pl.when(place == 0)
+            def _():
+                all_entering(micro, SEQ - 1).wait_send()
+
+            @pl.when(place > 0)
+            def _():
+                all_entering(micro, SEQ - 2).wait_send()
 
     with scope("second1"):
         join_second(1)
     with scope("finish1"):
         finish(1)
 
-    for micro in range(MICRO):
-        for which in (across_ring, after, behind, chip):
-            half(micro, which).wait_send()
-        for part in range(2):
-            send_before(micro, part).wait_send()
-            for way in range(2):
-                send_total(micro, way, part).wait_send()
-
-        @pl.when(section == 0)
-        def _():
-            for part in range(2):
-                handover(micro, part).wait_send()
+    every(halves.at[0], half_s.at[0], half_r.at[0]).wait_send()
+    every(before, before_s.at[0], before_r.at[0]).wait_send()
+    every(totals, total_s.at[0], total_r.at[0]).wait_send()
+
+    @pl.when(section == 0)
+    def _():
+        every(own, pipe_s.at[0], pipe_r.at[0]).wait_send()
 
 
 def shards(
@@ -637,10 +640,9 @@
             pltpu.VMEM((MICRO, SLAB, ROWS), BF16),
             pltpu.VMEM((MICRO, 2, SLAB, ROWS), BF16),
             pltpu.VMEM((MICRO, NARROW, ROWS), BF16),
-            dma(14), dma(MICRO * SENDS), dma(CHIPS * MICRO * 2), dma(CHIPS * MICRO), dma(MICRO), dma(MICRO),
-            dma(MICRO * SEQ), dma(MICRO * SEQ), dma(MICRO * SEQ), dma(MICRO * SEQ), dma(MICRO * SEQ), dma(MICRO * SEQ),
-            dma(MICRO * CHIPS), dma(MICRO * CHIPS), dma(MICRO * 2), dma(MICRO * 2), dma(MICRO * 4), dma(MICRO * 4),
-            dma(MICRO * 2), dma(MICRO * 2),
+            dma(14), dma(2), dma((NEAR + 1) * MICRO), dma(CHIPS * MICRO), dma(MICRO), dma(MICRO),
+            dma(MICRO), dma(MICRO), dma(MICRO), dma(MICRO), dma(MICRO), dma(MICRO),
+            dma(1), dma(MICRO * CHIPS), dma(1), dma(MICRO * 2), dma(1), dma(MICRO), dma(1), dma(MICRO),
         ],
         compiler_params=pltpu.CompilerParams(
             collective_id=0, has_side_effects=True, vmem_limit_bytes=56 * 1024 * 1024

time: 103 us -> 97.4 us (0.946)
  Pallas kernels: 102 us -> 96.7 us
    pallas_call x1, Pallas kernels: 102 us -> 96.7 us  [shards(): pl.pallas_call(kernel, out_shape=pltpu.VMEM((1, MICRO, NARROW, ROWS), BF1...]
where the time goes in v4:
time: 97.4 us
  Pallas kernels  96.7 us (99%)
    pallas_call x1, Pallas kernels, shards(): pl.pallas_call(kernel, out_shape=pltpu.VMEM((1, MICRO, NARROW, ROWS), BF1...  96.7 us

profile of v4, /device:TPU:6, one launch (start us, length us, event | category | flops | bytes accessed | tf_op | source)
XLA Modules:
  0.0 97.4 jit_solution(15002326987162673327)
XLA Ops:
  0.0 96.7 %shard_map.127 = bf16[1,2,320,128]{3,2,1,0:T(8,128)(2,1)S(1)} custom-call(bf16[2,320,128]{2,1,0:T(8,128)(2,1)} %bitcast.6, f32[1,2560]{1,0:T(1,128)} %pre_gain_h.1, bf16[1,2560,640]{2,1,0:T(8,128)(2,1)} %gate_h.1, bf16[1,2560,640]{2,1,0:T(8,128)(2,1)} %inner_h.1, bf16[1,2560,256]{2,1,0:T(8,128)(2,1)} %state_h.1, bf16[1,10,2560]{2,1,0:T(8,128)(2,1)} %bitcast.7, ...), custom_call_target="tpu_custom_call" | custom-call | tf_op jit(solution)/shard_map/pallas_call | solution.py:599
  96.7 0.7 copy.15

commit v5 on v4

--- a/solution.py
+++ b/solution.py
@@ -17,6 +17,7 @@
 LOCAL = INNER // SHARE
 STATE = 128
 BOTH = LOCAL + 2 * STATE
+WIDE = BOTH + 128
 HEADS = 10
 TAPS = 4
 SLAB = NARROW + 16
@@ -51,7 +52,7 @@
     tokens, pre_gain_h, gate_h, inner_h, state_h, step_h, inner_taps_h, state_taps_h, bias_h, rate_h, skip_h, gain_h,
     out_h, out,
     x, xg, w1, wd, wg, wo, pre_gain, inner_taps, state_taps, bias, rate, skip_scale, inner_gain,
-    acc, acc_d, gate_act, squares, scales, padded, inner_conv, state_conv, steps, sums, growth, mixed, decay, decays, sent,
+    acc, turned_steps, gate_act, squares, scales, padded, inner_conv, state_conv, steps, sums, growth, mixed, decay, decays, sent,
     arrived, back, entering, normed, halves, partner_half, joined, before, totals, own,
     local_s, gather_s, gather_r, share_r, rim_s, rim_r, decay_s, decay_r, state_s, state_r, enter_s, enter_r, half_s, half_r,
     before_s, before_r, total_s, total_r, pipe_s, pipe_r,
@@ -190,20 +191,25 @@
 
     def project(micro, which, first):
         shared(micro, which).wait_recv()
-        wide = x[which, micro].reshape(PAIR, ROWS).astype(F32).T
+        wide = x[which, micro].reshape(PAIR, ROWS).T.astype(F32)
         at = pl.ds(pl.multiple_of(which * PAIR, 128), PAIR)
         scaled = (wide * pre_gain[:, at]).astype(BF16)
         xg[micro, :, at] = scaled
         square = wide * wide
         square = sum(square[:, column : column + 128] for column in range(0, PAIR, 128))
         term = dot(scaled, w1[at, :])
-        term_d = dot_turned(scaled, wd[:, at])
         if first:
-            acc[micro], acc_d[micro], squares[micro] = term, term_d, square
+            acc[micro], squares[micro] = term, square
         else:
             acc[micro] += term
-            acc_d[micro] += term_d
             squares[micro] += square
+
+    def place_step_weights():
+        turned_steps[...] = jnp.zeros_like(turned_steps)
+        turned_steps[0:HEADS, :] = wd[...].astype(F32)
+        for column in range(0, WIDTH, 128):
+            at = slice(column, column + 128)
+            w1[at, BOTH : BOTH + 16] = turned_steps[:, at].T.astype(BF16)
 
     def rim(micro):
         return remote(
@@ -214,13 +220,13 @@
     def project_end(micro):
         scale = lax.rsqrt(jnp.sum(squares[micro], axis=1, keepdims=True) / WIDTH + EPS)
         scales[micro] = scale
-        padded[micro, EDGE : EDGE + ROWS, :] = (acc[micro] * scale).astype(BF16).astype(F32)
+        padded[micro, EDGE : EDGE + ROWS, :] = (acc[micro, :, 0:BOTH] * scale).astype(BF16).astype(F32)
 
         @pl.when(place < SEQ - 1)
         def _():
             rim(micro).start()
 
-        shifted = acc_d[micro] * scale + bias[...]
+        shifted = acc[micro, :, BOTH : BOTH + HEADS] * scale + bias[...]
         steps[micro, :, 0:HEADS] = jnp.maximum(shifted, 0.0) + jnp.log1p(jnp.exp(-jnp.abs(shifted)))
 
     row = lax.broadcasted_iota(jnp.int32, (ROWS, ROWS), 0)
@@ -485,39 +491,42 @@
         send_passed(0)
     for load in loads[MICRO:12]:
         load.wait()
+    place_step_weights()
     with scope("near0"):
         forward_near(0)
+    with scope("own1"):
+        send_passed(1)
     with scope("p0"):
         project(0, chip, True)
         project(0, behind, False)
-    with scope("own1"):
-        send_passed(1)
-        project(0, after, False)
 
     @pl.when(section == 0)
     def _():
         forward_near(1)
 
+    with scope("p0b"):
+        project(0, after, False)
     with scope("far0"):
         forward_far(0)
-        project(0, across_ring, False)
-        project_end(0)
 
     @pl.when(section == 1)
     def _():
         forward_near(1)
 
+    with scope("far0b"):
+        project(1, chip, True)
+        project(0, across_ring, False)
+        project_end(0)
     with scope("p1"):
-        project(1, chip, True)
         project(1, behind, False)
         project(1, after, False)
-    with scope("states0"):
-        states(0)
-        send_states(0)
     with scope("far1"):
         forward_far(1)
         project(1, across_ring, False)
         project_end(1)
+    with scope("states0"):
+        states(0)
+        send_states(0)
     for load in loads[12:]:
         load.wait()
     with scope("fill0"):
@@ -555,6 +564,7 @@
         join_direct(1, 0)
         spread(1, total1, chip)
         join_direct(1, 1)
+        join_second(1)
     with scope("finish0"):
         finish(0)
     with scope("sent"):
@@ -576,8 +586,6 @@
             def _():
                 all_entering(micro, SEQ - 2).wait_send()
 
-    with scope("second1"):
-        join_second(1)
     with scope("finish1"):
         finish(1)
 
@@ -604,7 +612,7 @@
         scratch_shapes=[
             pltpu.VMEM((CHIPS, MICRO, 2, NARROW, ROWS), BF16),
             pltpu.VMEM((MICRO, ROWS, WIDTH), BF16),
-            pltpu.VMEM((WIDTH, BOTH), BF16),
+            pltpu.VMEM((WIDTH, WIDE), BF16),
             pltpu.VMEM((HEADS, WIDTH), BF16),
             pltpu.VMEM((WIDTH, LOCAL), BF16),
             pltpu.VMEM((LOCAL, WIDTH), BF16),
@@ -615,8 +623,8 @@
             pltpu.VMEM((1, HEADS), F32),
             pltpu.VMEM((1, HEADS), F32),
             pltpu.VMEM((1, LOCAL), F32),
-            pltpu.VMEM((MICRO, ROWS, BOTH), F32),
-            pltpu.VMEM((MICRO, ROWS, HEADS), F32),
+            pltpu.VMEM((MICRO, ROWS, WIDE), F32),
+            pltpu.VMEM((16, WIDTH), F32),
             pltpu.VMEM((MICRO, ROWS, LOCAL), F32),
             pltpu.VMEM((MICRO, ROWS, 128), F32),
             pltpu.VMEM((MICRO, ROWS, 1), F32),

time: 97.4 us -> 88.8 us (0.912)
  Pallas kernels: 96.7 us -> 87.4 us
    pallas_call x1, Pallas kernels: 96.7 us -> 87.4 us  [shards(): pl.pallas_call(kernel, out_shape=pltpu.VMEM((1, MICRO, NARROW, ROWS), BF1...]
where the time goes in v5:
time: 88.8 us; the launch traced here: 88.1 us
  Pallas kernels  87.4 us (98%)
    pallas_call x1, Pallas kernels, shards(): pl.pallas_call(kernel, out_shape=pltpu.VMEM((1, MICRO, NARROW, ROWS), BF1...  87.4 us

profile of v5, /device:TPU:6, one launch (start us, length us, event | category | flops | bytes accessed | tf_op | source)
XLA Modules:
  0.0 88.1 jit_solution(16258183481018737727)
XLA Ops:
  0.0 87.4 %shard_map.127 = bf16[1,2,320,128]{3,2,1,0:T(8,128)(2,1)S(1)} custom-call(bf16[2,320,128]{2,1,0:T(8,128)(2,1)} %bitcast.6, f32[1,2560]{1,0:T(1,128)} %pre_gain_h.1, bf16[1,2560,640]{2,1,0:T(8,128)(2,1)} %gate_h.1, bf16[1,2560,640]{2,1,0:T(8,128)(2,1)} %inner_h.1, bf16[1,2560,256]{2,1,0:T(8,128)(2,1)} %state_h.1, bf16[1,10,2560]{2,1,0:T(8,128)(2,1)} %bitcast.7, ...), custom_call_target="tpu_custom_call" | custom-call | tf_op jit(solution)/shard_map/pallas_call | solution.py:607
  87.4 0.7 copy.15

commit v6 on v5

--- a/solution.py
+++ b/solution.py
@@ -22,6 +22,7 @@
 TAPS = 4
 SLAB = NARROW + 16
 OWNED = STATE // SEQ
+SOON = 4
 EDGE = 8
 HALF = NARROW // 2
 SENDS = 10
@@ -53,7 +54,7 @@
     out_h, out,
     x, xg, w1, wd, wg, wo, pre_gain, inner_taps, state_taps, bias, rate, skip_scale, inner_gain,
     acc, turned_steps, gate_act, squares, scales, padded, inner_conv, state_conv, steps, sums, growth, mixed, decay, decays, sent,
-    arrived, back, entering, normed, halves, partner_half, joined, before, totals, own,
+    arrived, back, entering, normed, halves, partner_half, joined, before, totals, partial, own,
     local_s, gather_s, gather_r, share_r, rim_s, rim_r, decay_s, decay_r, state_s, state_r, enter_s, enter_r, half_s, half_r,
     before_s, before_r, total_s, total_r, pipe_s, pipe_r,
 ):
@@ -87,14 +88,6 @@
         )
     ]
 
-    @pl.when(section == 0)
-    def _():
-        for load in loads[:MICRO]:
-            load.start()
-
-    for load in loads[MICRO:]:
-        load.start()
-
     barrier = pltpu.get_barrier_semaphore()
 
     def greet(peer):
@@ -106,6 +99,14 @@
     greet(device(after))
     greet(device(behind))
     greet({"tensor": partner})
+
+    @pl.when(section == 0)
+    def _():
+        for load in loads[:MICRO]:
+            load.start()
+
+    for load in loads[MICRO:]:
+        load.start()
 
     steps[...] = jnp.zeros_like(steps)
 
@@ -234,12 +235,32 @@
     first_half = lane < 64
     later = row >= lane
 
-    def states(micro):
+    distances = (4, 3, 5, 2, 6, 1, 7, 0)
+    others = [
+        lax.rem(place // 2 + step, SEQ // 2) * 2 + side
+        for step in distances
+        for side in range(2)
+    ]
+
+    def decay_to(micro, owner):
+        return remote(
+            decay.at[micro], decays.at[micro, place], decay_s.at[micro], decay_r.at[micro], {"seq": owner}
+        )
+
+    def prepare(micro):
         rates = jnp.concatenate([rate[...], jnp.zeros((1, 128 - HEADS), F32)], axis=1)
         step_size = steps[micro]
         cumulative = dot(later.astype(F32), -step_size * rates, precision=HIGHEST)
         sums[micro] = cumulative
         decay[micro] = jnp.exp(cumulative[ROWS - 1 :, :])
+        for owner in others:
+
+            @pl.when(jnp.logical_and(place != owner, place < SEQ - 1))
+            def _():
+                decay_to(micro, owner).start()
+
+    def states(micro):
+        step_size, cumulative = steps[micro], sums[micro]
 
         @pl.when(place > 0)
         def _():
@@ -272,21 +293,10 @@
             sent[micro, :, :, at] = state.reshape(SEQ, OWNED, 128).astype(BF16)
             growth[micro, :, at] = jnp.exp(each)
 
-    distances = (4, 3, 5, 2, 6, 1, 7, 0)
-    others = [
-        lax.rem(place // 2 + step, SEQ // 2) * 2 + side
-        for step in distances
-        for side in range(2)
-    ]
-
-    def decay_to(micro, owner):
-        return remote(
-            decay.at[micro], decays.at[micro, place], decay_s.at[micro], decay_r.at[micro], {"seq": owner}
-        )
-
     def state_to(micro, owner):
         return remote(
-            sent.at[micro, owner], arrived.at[micro, place], state_s.at[micro], state_r.at[micro], {"seq": owner}
+            sent.at[micro, owner], arrived.at[micro, place], state_s.at[micro],
+            state_r.at[micro * 2 + jnp.minimum(place // SOON, 1)], {"seq": owner}
         )
 
     def enter_to(micro, target):
@@ -298,9 +308,9 @@
         block = decays.at[micro, 0:count]
         return remote(block, block, decay_s.at[micro], decay_r.at[micro], to_partner)
 
-    def all_states(micro, count):
+    def all_states(micro, count, group=0):
         block = arrived.at[micro, 0:count]
-        return remote(block, block, state_s.at[micro], state_r.at[micro], to_partner)
+        return remote(block, block, state_s.at[micro], state_r.at[micro * 2 + group], to_partner)
 
     def all_entering(micro, count):
         block = entering.at[micro, 0:count]
@@ -311,7 +321,6 @@
 
             @pl.when(jnp.logical_and(place != owner, place < SEQ - 1))
             def _():
-                decay_to(micro, owner).start()
                 state_to(micro, owner).start()
 
     def gate(micro):
@@ -344,23 +353,39 @@
         @pl.when(place < SEQ - 1)
         def _():
             all_decays(micro, SEQ - 2).wait_recv()
-            all_states(micro, SEQ - 2).wait_recv()
 
         @pl.when(place == SEQ - 1)
         def _():
             all_decays(micro, SEQ - 1).wait_recv()
-            all_states(micro, SEQ - 1).wait_recv()
 
         rows = jnp.concatenate([decays[micro, source] for source in range(SEQ)], axis=0)
         factors = dot(rows, expand, precision=HIGHEST)
+
         carried = jnp.zeros((OWNED, LOCAL), F32)
-        for source in range(SEQ - 1):
-            carried = factors[source : source + 1, :] * carried + arrived[micro, source].astype(F32)
-            back[micro, source + 1] = carried.astype(BF16)
+        for group, (begin, end) in enumerate(((0, SOON), (SOON, SEQ - 1))):
+            inside_group = jnp.logical_and(place >= begin, place < end)
+
+            @pl.when(inside_group)
+            def _():
+                all_states(micro, end - begin - 1, group).wait_recv()
+
+            @pl.when(jnp.logical_not(inside_group))
+            def _():
+                all_states(micro, end - begin, group).wait_recv()
+
+            for source in range(begin, end):
+                carried = factors[source : source + 1, :] * carried + arrived[micro, source].astype(F32)
+                back[micro, source + 1] = carried.astype(BF16)
+            if group == 0:
+                for target in range(1, SOON + 1):
+
+                    @pl.when(place != target)
+                    def _():
+                        enter_to(micro, target).start()
 
         for target in others:
 
-            @pl.when(jnp.logical_and(place != target, target > 0))
+            @pl.when(jnp.logical_and(place != target, target > SOON))
             def _():
                 enter_to(micro, target).start()
 
@@ -468,9 +493,15 @@
             pack(micro, which, part, added(value, unpacked(before[micro, PARTS[part]], part)))
             send_total(micro, part, part).start()
 
-    def finish(micro):
+    def join_own(micro):
         half(micro, chip).wait_recv()
         values = [join(micro, chip, part) for part in range(2)]
+        partial[micro, EARLY, :] = values[0][0]
+        partial[micro, LATE, :] = values[1][0]
+        partial[micro, NARROW : NARROW + 1, :] = values[1][1]
+
+    def finish(micro):
+        values = [(partial[micro, EARLY, :],), (partial[micro, LATE, :], partial[micro, NARROW : NARROW + 1, :])]
         every(totals.at[micro], total_s.at[0], total_r.at[micro]).wait_recv()
         for way, part in ((0, 1), (1, 0), (0, 0), (1, 1)):
             values[part] = added(values[part], unpacked(totals[micro, way, PARTS[part]], part))
@@ -492,12 +523,17 @@
     for load in loads[MICRO:12]:
         load.wait()
     place_step_weights()
+    project(0, chip, True)
+
+    @pl.when(section == 0)
+    def _():
+        project(1, chip, True)
+
     with scope("near0"):
         forward_near(0)
     with scope("own1"):
         send_passed(1)
     with scope("p0"):
-        project(0, chip, True)
         project(0, behind, False)
 
     @pl.when(section == 0)
@@ -512,16 +548,25 @@
     @pl.when(section == 1)
     def _():
         forward_near(1)
+        project(1, chip, True)
 
     with scope("far0b"):
-        project(1, chip, True)
         project(0, across_ring, False)
         project_end(0)
+    @pl.when(section == 0)
+    def _():
+        forward_far(1)
+
     with scope("p1"):
         project(1, behind, False)
         project(1, after, False)
+
+    @pl.when(section == 1)
+    def _():
+        forward_far(1)
+
+    prepare(0)
     with scope("far1"):
-        forward_far(1)
         project(1, across_ring, False)
         project_end(1)
     with scope("states0"):
@@ -530,12 +575,13 @@
     for load in loads[12:]:
         load.wait()
     with scope("fill0"):
+        prepare(1)
         gate(0)
-        inside(0)
     with scope("states1"):
         states(1)
         send_states(1)
     with scope("fill1"):
+        inside(0)
         gate(1)
         inside(1)
     with scope("scan0"):
@@ -557,13 +603,15 @@
         spread(1, total1, after)
         join_direct(0, 1)
         join_before(1)
+        join_second(0)
         spread(0, total, chip)
     with scope("second0"):
-        join_second(0)
         spread(1, total1, behind)
         join_direct(1, 0)
         spread(1, total1, chip)
         join_direct(1, 1)
+        join_own(0)
+        join_own(1)
         join_second(1)
     with scope("finish0"):
         finish(0)
@@ -647,9 +695,10 @@
             pltpu.VMEM((MICRO, CHIPS, SLAB, ROWS), BF16),
             pltpu.VMEM((MICRO, SLAB, ROWS), BF16),
             pltpu.VMEM((MICRO, 2, SLAB, ROWS), BF16),
+            pltpu.VMEM((MICRO, NARROW + 8, ROWS), F32),
             pltpu.VMEM((MICRO, NARROW, ROWS), BF16),
             dma(14), dma(2), dma((NEAR + 1) * MICRO), dma(CHIPS * MICRO), dma(MICRO), dma(MICRO),
-            dma(MICRO), dma(MICRO), dma(MICRO), dma(MICRO), dma(MICRO), dma(MICRO),
+            dma(MICRO), dma(MICRO), dma(MICRO), dma(MICRO * 2), dma(MICRO), dma(MICRO),
             dma(1), dma(MICRO * CHIPS), dma(1), dma(MICRO * 2), dma(1), dma(MICRO), dma(1), dma(MICRO),
         ],
         compiler_params=pltpu.CompilerParams(

time: 88.8 us -> 87.4 us (0.984)
  Pallas kernels: 87.4 us -> 86.5 us
    pallas_call x1, Pallas kernels: 87.4 us -> 86.5 us  [shards(): pl.pallas_call(kernel, out_shape=pltpu.VMEM((1, MICRO, NARROW, ROWS), BF1...]
where the time goes in v6:
time: 87.4 us; the launch traced here: 87.1 us
  Pallas kernels  86.5 us (99%)
    pallas_call x1, Pallas kernels, shards(): pl.pallas_call(kernel, out_shape=pltpu.VMEM((1, MICRO, NARROW, ROWS), BF1...  86.5 us

profile of v6, /device:TPU:6, one launch (start us, length us, event | category | flops | bytes accessed | tf_op | source)
XLA Modules:
  0.0 87.1 jit_solution(3960186031362576810)
XLA Ops:
  0.0 86.5 %shard_map.127 = bf16[1,2,320,128]{3,2,1,0:T(8,128)(2,1)S(1)} custom-call(bf16[2,320,128]{2,1,0:T(8,128)(2,1)} %bitcast.6, f32[1,2560]{1,0:T(1,128)} %pre_gain_h.1, bf16[1,2560,640]{2,1,0:T(8,128)(2,1)} %gate_h.1, bf16[1,2560,640]{2,1,0:T(8,128)(2,1)} %inner_h.1, bf16[1,2560,256]{2,1,0:T(8,128)(2,1)} %state_h.1, bf16[1,10,2560]{2,1,0:T(8,128)(2,1)} %bitcast.7, ...), custom_call_target="tpu_custom_call" | custom-call | tf_op jit(solution)/shard_map/pallas_call | solution.py:655
  86.5 0.7 copy.15

commit v7 on v6

--- a/solution.py
+++ b/solution.py
@@ -296,7 +296,7 @@
     def state_to(micro, owner):
         return remote(
             sent.at[micro, owner], arrived.at[micro, place], state_s.at[micro],
-            state_r.at[micro * 2 + jnp.minimum(place // SOON, 1)], {"seq": owner}
+            state_r.at[micro * 3 + jnp.minimum(place // SOON, 2)], {"seq": owner}
         )
 
     def enter_to(micro, target):
@@ -310,7 +310,7 @@
 
     def all_states(micro, count, group=0):
         block = arrived.at[micro, 0:count]
-        return remote(block, block, state_s.at[micro], state_r.at[micro * 2 + group], to_partner)
+        return remote(block, block, state_s.at[micro], state_r.at[micro * 3 + group], to_partner)
 
     def all_entering(micro, count):
         block = entering.at[micro, 0:count]
@@ -362,7 +362,7 @@
         factors = dot(rows, expand, precision=HIGHEST)
 
         carried = jnp.zeros((OWNED, LOCAL), F32)
-        for group, (begin, end) in enumerate(((0, SOON), (SOON, SEQ - 1))):
+        for group, (begin, end) in enumerate(((0, SOON), (SOON, 2 * SOON), (2 * SOON, SEQ - 1))):
             inside_group = jnp.logical_and(place >= begin, place < end)
 
             @pl.when(inside_group)
@@ -376,8 +376,8 @@
             for source in range(begin, end):
                 carried = factors[source : source + 1, :] * carried + arrived[micro, source].astype(F32)
                 back[micro, source + 1] = carried.astype(BF16)
-            if group == 0:
-                for target in range(1, SOON + 1):
+            if group < 2:
+                for target in range(begin + 1, end + 1):
 
                     @pl.when(place != target)
                     def _():
@@ -385,7 +385,7 @@
 
         for target in others:
 
-            @pl.when(jnp.logical_and(place != target, target > SOON))
+            @pl.when(jnp.logical_and(place != target, target > 2 * SOON))
             def _():
                 enter_to(micro, target).start()
 
@@ -698,7 +698,7 @@
             pltpu.VMEM((MICRO, NARROW + 8, ROWS), F32),
             pltpu.VMEM((MICRO, NARROW, ROWS), BF16),
             dma(14), dma(2), dma((NEAR + 1) * MICRO), dma(CHIPS * MICRO), dma(MICRO), dma(MICRO),
-            dma(MICRO), dma(MICRO), dma(MICRO), dma(MICRO * 2), dma(MICRO), dma(MICRO),
+            dma(MICRO), dma(MICRO), dma(MICRO), dma(MICRO * 3), dma(MICRO), dma(MICRO),
             dma(1), dma(MICRO * CHIPS), dma(1), dma(MICRO * 2), dma(1), dma(MICRO), dma(1), dma(MICRO),
         ],
         compiler_params=pltpu.CompilerParams(

time: 87.4 us -> 88.6 us (1.014)
  Pallas kernels: 86.5 us -> 87.5 us
    pallas_call x1, Pallas kernels: 86.5 us -> 87.5 us  [shards(): pl.pallas_call(kernel, out_shape=pltpu.VMEM((1, MICRO, NARROW, ROWS), BF1...]
where the time goes in v7:
time: 88.6 us; the launch traced here: 88.2 us
  Pallas kernels  87.5 us (99%)
    pallas_call x1, Pallas kernels, shards(): pl.pallas_call(kernel, out_shape=pltpu.VMEM((1, MICRO, NARROW, ROWS), BF1...  87.5 us

profile of v7, /device:TPU:6, one launch (start us, length us, event | category | flops | bytes accessed | tf_op | source)
XLA Modules:
  0.0 88.2 jit_solution(5710828653964519209)
XLA Ops:
  0.0 87.5 %shard_map.127 = bf16[1,2,320,128]{3,2,1,0:T(8,128)(2,1)S(1)} custom-call(bf16[2,320,128]{2,1,0:T(8,128)(2,1)} %bitcast.6, f32[1,2560]{1,0:T(1,128)} %pre_gain_h.1, bf16[1,2560,640]{2,1,0:T(8,128)(2,1)} %gate_h.1, bf16[1,2560,640]{2,1,0:T(8,128)(2,1)} %inner_h.1, bf16[1,2560,256]{2,1,0:T(8,128)(2,1)} %state_h.1, bf16[1,10,2560]{2,1,0:T(8,128)(2,1)} %bitcast.7, ...), custom_call_target="tpu_custom_call" | custom-call | tf_op jit(solution)/shard_map/pallas_call | solution.py:655
  87.5 0.7 copy.15
